TPU v7x, 256 devices: a whole 4x4x8 slice. The times are simulated.
256 devices in a mesh: view: 8 (over x, core), gauss: 32 (over y, z).
Axes of the slice: x: 4, y: 4, z: 8, core: 2. Of those that a mesh axis runs over, the one named last changes fastest.
Arguments:
- means: float32 [3, 524288], P(None, 'gauss'), may hold values from -1 to 1
- scales: float32 [3, 524288], P(None, 'gauss'), may hold values from 0.05 to 0.6
- quats: float32 [4, 524288], P(None, 'gauss'), may hold values from -6 to 6
- attrs: float32 [49, 524288], P(None, 'gauss'), may hold values from -6 to 6
- grad_screen: float32 [32, 2, 524288], P('view', None, 'gauss'), may hold values from -6 to 6
- visible: int32 [32, 524288], P('view', 'gauss'), may hold values 0 or 1
- clone_mask: int32 [524288], P('gauss'), may hold values from 0 to 1, as said below
- rotation: float32 [32, 3, 3], P('view'), may hold values from -3.5 to 3.5
- shift: float32 [32, 3], P('view'), may hold values from 2 to 5
- focal: float32 [32], P('view'), may hold values from 1 to 4
Outputs:
- peak_stats: float32 [2, 524288], P(None, 'gauss')
- clones: float32 [61, 524288], P(None, 'gauss')
- clone_total: int32 [], replicated
Inputs may be any that keep to these rules, and one draw needn't show every extreme that they name: `clone_mask`: in every draw some shard of 16384 consecutive Gaussians has all of them marked.
All inputs are finite; a program needn't handle non-finite values. No bound on the sum of `visible` on one device may be relied on, other than what follows from the above.
Results may differ from a plain program's by a relative error of at most 0.0003.
Values sent between devices are 32-bit elements; how exact they have to be, the bound alone decides.
A program may use at most 128 MiB of HBM per device.

v0:
```python
import jax
import jax.numpy as jnp
from jax import lax
from jax.sharding import PartitionSpec as P

G_DEV = 16384


def copy_for_each(x, axis):
    count = lax.axis_size(axis)
    return lax.all_to_all(jnp.broadcast_to(x[None], (count, *x.shape)), axis, 0, 0, tiled=True)


def of_everyone(x, axis):
    return copy_for_each(x, axis).max(axis=0)


def together(arrays, axis):
    vector, at, done = (jnp.concatenate([a.reshape(-1) for a in arrays]), 0, [])
    running = of_everyone(vector, axis)
    for a in arrays:
        done.append(running[at : at + a.size].reshape(a.shape))
        at += a.size
    return tuple(done)


def folded_in_pairs(pieces, combine):
    while len(jax.tree.leaves(pieces)[0]) > 1:
        pieces = jax.vmap(combine)(*(pieces[side::2] for side in (0, 1)))
    return pieces[0]


def prefix(x, axis, combine, identity):
    count, mine = (lax.axis_size(axis), lax.axis_index(axis))
    passed = jnp.arange(count) < mine

    def kept(part, zero, own):
        part = jnp.where(
            passed.reshape(-1, *(1 for _ in own.shape)), part, jnp.asarray(zero, own.dtype)
        )
        return part

    pieces = copy_for_each(x, axis)
    return folded_in_pairs(kept(pieces, identity, x), combine)


def of_everyone_2(x, axis):
    everything = copy_for_each(x, axis)
    return jnp.sum(everything, axis=0)


def quat_factor(scales, quats):
    inv = 1.0 / jnp.sqrt(jnp.sum(quats * quats, axis=0) + 0.25)
    w, x, y, z = (quats[0] * inv, quats[1] * inv, quats[2] * inv, quats[3] * inv)
    rq = [
        [1 - 2 * (y * y + z * z), 2 * (x * y - w * z), 2 * (x * z + w * y)],
        [2 * (x * y + w * z), 1 - 2 * (x * x + z * z), 2 * (y * z - w * x)],
        [2 * (x * z - w * y), 2 * (y * z + w * x), 1 - 2 * (x * x + y * y)],
    ]
    return [[rq[i][j] * scales[j] for j in range(3)] for i in range(3)]


def view_stats(means, factor, grad, seen, rot, trans, focal_v):
    point = [
        rot[i, 0] * means[0] + rot[i, 1] * means[1] + rot[i, 2] * means[2] + trans[i]
        for i in range(3)
    ]
    depth = jnp.maximum(point[2], 1.0)
    j00 = focal_v / depth
    j02 = -focal_v * point[0] / (depth * depth)
    j12 = -focal_v * point[1] / (depth * depth)
    first = [j00 * rot[0, j] + j02 * rot[2, j] for j in range(3)]
    second = [j00 * rot[1, j] + j12 * rot[2, j] for j in range(3)]
    prow = [sum((first[j] * factor[j][k] for j in range(3))) for k in range(3)]
    qrow = [sum((second[j] * factor[j][k] for j in range(3))) for k in range(3)]
    a_val = prow[0] ** 2 + prow[1] ** 2 + prow[2] ** 2 + 0.3
    c_val = qrow[0] ** 2 + qrow[1] ** 2 + qrow[2] ** 2 + 0.3
    b_val = prow[0] * qrow[0] + prow[1] * qrow[1] + prow[2] * qrow[2]
    half = 0.5 * (a_val - c_val)
    lam = 0.5 * (a_val + c_val) + jnp.sqrt(half * half + b_val * b_val + 0.01)
    seenf = seen.astype(jnp.float32)
    radius = 3.0 * jnp.sqrt(lam) * seenf
    gnorm = jnp.sqrt(grad[0] * grad[0] + grad[1] * grad[1]) * seenf
    return (gnorm, radius)


def add_ints(earlier, later):
    return earlier + later


def body(means, scales, quats, attrs, grad_screen, visible, clone_mask, rotation, shift, focal):
    factor = quat_factor(scales, quats)
    gmax = jnp.zeros(means.shape[1], jnp.float32)
    rmax = jnp.zeros(means.shape[1], jnp.float32)
    for v in range(grad_screen.shape[0]):
        gnorm, radius = view_stats(
            means, factor, grad_screen[v], visible[v], rotation[v], shift[v], focal[v]
        )
        gmax = jnp.maximum(gmax, gnorm)
        rmax = jnp.maximum(rmax, radius)
    gmax, rmax = together((gmax, rmax), "view")
    peak = jnp.stack([gmax, rmax])
    rows = jnp.concatenate([means, scales, quats, attrs, peak], axis=0)
    feat_rows = rows.shape[0]
    shards = lax.axis_size("gauss")
    cap_blk = G_DEV // 128
    count = jnp.sum(clone_mask)
    blocks = (count + 127) // 128
    offset = prefix(blocks, "gauss", add_ints, jnp.int32(0))
    summed = of_everyone_2(count.astype(jnp.float32), "gauss")
    total = summed.astype(jnp.int32)
    rank = jnp.cumsum(clone_mask) - 1
    where_to = jnp.where(clone_mask == 1, rank, cap_blk * 128)
    packed = (
        jnp.zeros((feat_rows, cap_blk * 128), jnp.float32).at[:, where_to].set(rows, mode="drop")
    )
    packed = packed.reshape(feat_rows, cap_blk, 128)
    per = (cap_blk + shards - 1) // shards
    target = jnp.arange(shards, dtype=jnp.int32)[:, None]
    within = jnp.arange(per, dtype=jnp.int32)[None, :]
    local_blk = (target - offset) % shards + within * shards
    valid = local_blk < blocks
    picked = jnp.minimum(local_blk, cap_blk - 1).reshape(-1)
    outgoing = packed[:, picked, :] * valid.reshape(1, -1, 1).astype(jnp.float32)
    outgoing = outgoing.reshape(feat_rows, shards, per, 128)
    slot_ids = (
        jnp.where(valid, (offset + local_blk) // shards, cap_blk)
        .astype(jnp.int32)
        .reshape(1, shards, per)
    )
    width = 128 // lax.axis_size("view")
    start = lax.axis_index("view") * width
    portion = lax.dynamic_slice_in_dim(outgoing, start, width, 3)
    arrived, slots_in = (
        lax.all_to_all(portion, "gauss", split_axis=1, concat_axis=1, tiled=True),
        lax.all_to_all(slot_ids, "gauss", split_axis=1, concat_axis=1, tiled=True),
    )
    arrived = arrived.reshape(feat_rows, shards * per, width)
    partial_place = (
        jnp.zeros((feat_rows, cap_blk, width), jnp.float32)
        .at[:, slots_in.reshape(-1)]
        .set(arrived, mode="drop")
    )
    placed = lax.all_gather(partial_place, "view", axis=2, tiled=True)
    clones = placed.reshape(feat_rows, cap_blk * 128)
    return (peak, clones, total)


def solution(mesh):
    return jax.shard_map(
        body,
        mesh=mesh,
        in_specs=(
            P(None, "gauss"),
            P(None, "gauss"),
            P(None, "gauss"),
            P(None, "gauss"),
            P("view", None, "gauss"),
            P("view", "gauss"),
            P("gauss"),
            P("view", None, None),
            P("view", None),
            P("view"),
        ),
        out_specs=(P(None, "gauss"), P(None, "gauss"), P()),
        check_vma=False,
    )
```

profile of v0, /device:TPU:1, one launch (start us, length us, event | category | flops | bytes accessed | tf_op | source)
XLA Modules:
  0.0 326.7 jit_solution(10295088173397887772)
XLA Ops:
  7.2 1.0 copy.37
  8.2 0.2 reduce-window.9
  8.4 0.1 copy.38
  8.5 0.2 reduce-window.12
  8.9 2.1 compare_select_fusion
  11.6 0.6 broadcast_in_dim.45
  12.2 12.0 %all-to-all-start.1 = ((s32[32,1,1]{2,1,0:T(1,128)}), s32[32,1,1]{2,1,0:T(1,128)S(1)}, u32[]{:S(2)}, u32[]{:S(2)}) async-start(s32[32,1,1]{2,1,0:T(1,128)} %broadcast_in_dim.45), calls=%async_computation.1 | async-start | bytes 32768 | tf_op jit(solution)/shard_map/all_to_all | solution.py:11
  24.2 2.4 fusion.6
  26.7 1.1 multiply_reduce_fusion
  27.8 0.6 iota_multiply_fusion
  28.4 0.8 fusion.9
  29.2 0.7 fusion.10
  29.9 1.8 fusion.11
  31.7 1.5 fusion.16
  33.8 7.2 %multiply_add_fusion.23 = (f32[1,16384]{1,0:T(1,128)S(1)}, f32[1,16384]{1,0:T(1,128)S(1)}, f32[1,16384]{1,0:T(1,128)S(1)}, f32[1,16384]{1,0:T(1,128)S(1)}) fusion(f32[]{:T(128)} %bitcast.13, f32[]{:T(128)} %bitcast.9, f32[]{:T(128)} %bitcast.16, f32[3,16384]{1,0:T(4,128)} %param.10, f32[]{:T(128)} %bitcast.15, f32[]{:T(128)} %bitcast.14, f32[]{:T(128)S(6)} %neg.16, ...), kind=kLoop, calls=%fused_computation.35 | loop fusion | flops 327680 | bytes 458792 | tf_op jit(solution)/shard_map/add | solution.py:72
  41.1 7.3 %multiply_add_fusion.22 = (f32[1,16384]{1,0:T(1,128)S(1)}, f32[1,16384]{1,0:T(1,128)S(1)}, f32[1,16384]{1,0:T(1,128)S(1)}, f32[1,16384]{1,0:T(1,128)S(1)}) fusion(f32[1,16384]{1,0:T(1,128)S(1)} %get-tuple-element.22, f32[1,16384]{1,0:T(1,128)S(1)} %get-tuple-element.23, f32[]{:T(128)} %bitcast.14, f32[]{:T(128)} %bitcast.10, f32[]{:T(128)} %bitcast.11, ...), kind=kLoop, calls=%fused_computation.34 | loop fusion | flops 294912 | bytes 655400 | tf_op jit(solution)/shard_map/add | solution.py:72
  48.3 2.5 multiply_add_fusion.19
  50.9 0.7 fusion.12
  52.2 7.4 %multiply_add_fusion.17 = (f32[1,16384]{1,0:T(1,128)S(1)}, f32[1,16384]{1,0:T(1,128)S(1)}, f32[1,16384]{1,0:T(1,128)S(1)}, f32[1,16384]{1,0:T(1,128)S(1)}) fusion(f32[]{:T(128)} %bitcast.39, f32[]{:T(128)} %bitcast.35, f32[]{:T(128)} %bitcast.42, f32[3,16384]{1,0:T(4,128)} %param.10, f32[]{:T(128)} %bitcast.41, f32[]{:T(128)} %bitcast.40, f32[]{:T(128)S(6)} %neg.17, ...), kind=kLoop, calls=%fused_computation.29 | loop fusion | flops 327680 | bytes 458792 | tf_op jit(solution)/shard_map/add | solution.py:72
  59.6 7.2 %multiply_add_fusion.16 = (f32[1,16384]{1,0:T(1,128)S(1)}, f32[1,16384]{1,0:T(1,128)S(1)}, f32[1,16384]{1,0:T(1,128)S(1)}, f32[1,16384]{1,0:T(1,128)S(1)}) fusion(f32[1,16384]{1,0:T(1,128)S(1)} %get-tuple-element.28, f32[1,16384]{1,0:T(1,128)S(1)} %get-tuple-element.29, f32[]{:T(128)} %bitcast.40, f32[]{:T(128)} %bitcast.36, f32[]{:T(128)} %bitcast.37, ...), kind=kLoop, calls=%fused_computation.28 | loop fusion | flops 294912 | bytes 655400 | tf_op jit(solution)/shard_map/add | solution.py:72
  66.8 2.5 multiply_add_fusion.13
  69.4 0.7 fusion.13
  70.7 7.4 %multiply_add_fusion.11 = (f32[1,16384]{1,0:T(1,128)S(1)}, f32[1,16384]{1,0:T(1,128)S(1)}, f32[1,16384]{1,0:T(1,128)S(1)}, f32[1,16384]{1,0:T(1,128)S(1)}) fusion(f32[]{:T(128)} %bitcast.58, f32[]{:T(128)} %bitcast.54, f32[]{:T(128)} %bitcast.61, f32[3,16384]{1,0:T(4,128)} %param.10, f32[]{:T(128)} %bitcast.60, f32[]{:T(128)} %bitcast.59, f32[]{:T(128)S(6)} %neg.18, ...), kind=kLoop, calls=%fused_computation.23 | loop fusion | flops 327680 | bytes 458792 | tf_op jit(solution)/shard_map/add | solution.py:72
  78.1 7.4 %multiply_add_fusion.10 = (f32[1,16384]{1,0:T(1,128)S(1)}, f32[1,16384]{1,0:T(1,128)S(1)}, f32[1,16384]{1,0:T(1,128)S(1)}, f32[1,16384]{1,0:T(1,128)S(1)}) fusion(f32[1,16384]{1,0:T(1,128)S(1)} %get-tuple-element.34, f32[1,16384]{1,0:T(1,128)S(1)} %get-tuple-element.35, f32[]{:T(128)} %bitcast.59, f32[]{:T(128)} %bitcast.55, f32[]{:T(128)} %bitcast.56, ...), kind=kLoop, calls=%fused_computation.22 | loop fusion | flops 294912 | bytes 655400 | tf_op jit(solution)/shard_map/add | solution.py:72
  85.4 2.6 multiply_add_fusion.7
  88.0 0.7 fusion.14
  89.4 7.4 %multiply_add_fusion.5 = (f32[1,16384]{1,0:T(1,128)S(1)}, f32[1,16384]{1,0:T(1,128)S(1)}, f32[1,16384]{1,0:T(1,128)S(1)}, f32[1,16384]{1,0:T(1,128)S(1)}) fusion(f32[]{:T(128)} %bitcast.77, f32[]{:T(128)} %bitcast.73, f32[]{:T(128)} %bitcast.80, f32[3,16384]{1,0:T(4,128)} %param.10, f32[]{:T(128)} %bitcast.79, f32[]{:T(128)} %bitcast.78, f32[]{:T(128)S(6)} %neg.19, ...), kind=kLoop, calls=%fused_computation.17 | loop fusion | flops 327680 | bytes 458792 | tf_op jit(solution)/shard_map/add | solution.py:72
  96.8 7.4 %multiply_add_fusion.4 = (f32[1,16384]{1,0:T(1,128)S(1)}, f32[1,16384]{1,0:T(1,128)S(1)}, f32[1,16384]{1,0:T(1,128)S(1)}, f32[1,16384]{1,0:T(1,128)S(1)}) fusion(f32[1,16384]{1,0:T(1,128)S(1)} %get-tuple-element.40, f32[1,16384]{1,0:T(1,128)S(1)} %get-tuple-element.41, f32[]{:T(128)} %bitcast.78, f32[]{:T(128)} %bitcast.74, f32[]{:T(128)} %bitcast.75, ...), kind=kLoop, calls=%fused_computation.16 | loop fusion | flops 294912 | bytes 655400 | tf_op jit(solution)/shard_map/add | solution.py:72
  104.2 2.6 multiply_add_fusion.1
  106.7 1.8 slice_convert_fusion.3
  108.5 0.8 fusion.7
  109.3 0.8 add_sqrt_fusion.3
  110.2 1.8 multiply_maximum_fusion
  112.0 1.5 broadcast_in_dim.24
  113.5 5.3 %all-to-all-start = ((f32[8,1,32768]{2,1,0:T(1,128)}), f32[8,1,32768]{2,1,0:T(1,128)S(1)}, u32[]{:S(2)}, u32[]{:S(2)}) async-start(f32[8,1,32768]{2,1,0:T(1,128)} %broadcast_in_dim.24), calls=%async_computation | async-start | bytes 2097152 | tf_op jit(solution)/shard_map/all_to_all | solution.py:11
  118.8 0.7 reduce.2
  119.4 0.1 slice.502
  120.3 0.6 fusion.15
  122.2 0.7 add_minimum_fusion
  123.0 0.7 fusion.2
  123.8 1.4 compare_select_fusion.1
  125.2 8.5 %all-to-all-done = f32[8,1,32768]{2,1,0:T(1,128)S(1)} async-done(((f32[8,1,32768]{2,1,0:T(1,128)}), f32[8,1,32768]{2,1,0:T(1,128)S(1)}, u32[]{:S(2)}, u32[]{:S(2)}) %all-to-all-start) | async-done | bytes 1048608 | tf_op jit(solution)/shard_map/all_to_all | solution.py:11
  133.7 9.7 %all-to-all-start.2 = ((s32[1,32,4]{2,0,1:T(1,128)}), s32[1,32,4]{2,0,1:T(1,128)S(1)}, u32[]{:S(2)}, u32[]{:S(2)}) async-start(s32[1,32,4]{2,0,1:T(1,128)} %compare_select_fusion.1), calls=%async_computation.2 | async-start | bytes 32768 | tf_op jit(solution)/shard_map/all_to_all | solution.py:136
  143.4 0.8 reduce_max.9
  144.2 21.5 %concatenate.8 = f32[61,16384]{1,0:T(8,128)} concatenate(f32[3,16384]{1,0:T(4,128)S(1)} %copy-done.1, f32[3,16384]{1,0:T(4,128)S(1)} %copy-done.3, f32[4,16384]{1,0:T(4,128)S(1)} %copy-done.2, f32[49,16384]{1,0:T(8,128)} %param.13, f32[1,16384]{1,0:T(1,128)S(1)} %bitcast.129, f32[1,16384]{1,0:T(1,128)S(1)} %bitcast.131), dimensions={0} | concatenate | bytes 7995392 | tf_op jit(solution)/shard_map/concatenate | solution.py:103
  165.8 6.9 %copy.40 = f32[16384,61]{1,0:T(8,128)} copy(f32[16384,61]{0,1:T(8,128)} %bitcast.126) | data formatting | bytes 7995392 | tf_op jit(solution)/shard_map/concatenate | solution.py:103
  172.7 44.3 %scatter_custom_fusion = f32[61,16384]{0,1:T(8,128)} fusion(s32[16384]{0:T(1024)} %get-tuple-element.78, f32[16384,61]{1,0:T(8,128)} %copy.40, f32[]{:T(128)} %constant.32.clone.1), kind=kCustom, calls=%fused_computation.3 | custom fusion | bytes 3998208 | tf_op jit(solution)/shard_map/scatter | solution.py:115
  217.0 7.7 %gather_fusion = f32[128,61,128]{1,2,0:T(8,128)} fusion(f32[61,128,128]{0,2,1:T(8,128)} %bitcast.125, s32[1024]{0:T(1024)S(1)} %pad_clamp_fusion), kind=kCustom, calls=%fused_computation | custom fusion | bytes 7995904 | tf_op jit(solution)/shard_map/gather | solution.py:124
  224.7 1.4 fusion.17
  226.2 2.3 reshape.640
  228.5 9.1 %all-to-all-start.3 = ((f32[32,1,3904]{2,1,0:T(1,128)}), f32[32,1,3904]{2,1,0:T(1,128)S(1)}, u32[]{:S(2)}, u32[]{:S(2)}) async-start(f32[32,1,3904]{2,1,0:T(1,128)} %reshape.640), calls=%async_computation.3 | async-start | bytes 1015808 | tf_op jit(solution)/shard_map/all_to_all | solution.py:135
  237.6 0.5 broadcast.525
  238.1 0.7 reduce.8
  238.9 11.3 %all-to-all-done.3 = f32[32,1,3904]{2,1,0:T(1,128)S(1)} async-done(((f32[32,1,3904]{2,1,0:T(1,128)}), f32[32,1,3904]{2,1,0:T(1,128)S(1)}, u32[]{:S(2)}, u32[]{:S(2)}) %all-to-all-start.3) | async-done | bytes 499744 | tf_op jit(solution)/shard_map/all_to_all | solution.py:135
  250.3 0.5 broadcast.551
  250.8 1.8 reduce.9
  252.6 1.5 reshape.641
  254.2 4.6 %scatter_fusion = f32[61,128,16]{0,2,1:T(8,128)S(1)} fusion(f32[61,128,16]{0,2,1:T(8,128)S(1)} %broadcast_in_dim.44, s32[128]{0:T(128)S(1)} %fusion.4, f32[128,61,16]{1,2,0:T(8,128)S(1)} %bitcast.124), kind=kCustom, calls=%fused_computation.2 | custom fusion | bytes 1499648 | tf_op jit(solution)/shard_map/scatter | solution.py:142
  258.8 1.0 copy-done
  260.4 16.9 %all_to_all.31 = f32[32,1,1]{2,1,0:T(1,128)S(1)} all-to-all(f32[32,1,1]{2,1,0:T(1,128)S(1)} %broadcast_in_dim.51), channel_id=1, replica_groups=mesh['view'=8,'gauss'=32] {'gauss'}, dimensions={0} | all-to-all | bytes 256 | tf_op jit(solution)/shard_map/all_to_all | solution.py:11
  277.3 0.6 reduce_sum.29
  278.6 0.8 pad_maximum_fusion.1
  279.4 32.5 %all-gather.2.cloned.1.call-done = f32[61,128,128]{0,2,1:T(8,128)} async-done(((f32[61,128,16]{0,2,1:T(8,128)}), f32[61,128,128]{0,2,1:T(8,128)}) %all-gather.2.cloned.1.call-update) | async-done | bytes 3997712 | tf_op jit(solution)/shard_map/all_gather | solution.py:144
  311.9 6.8 %copy.42 = f32[61,16384]{1,0:T(8,128)} copy(f32[61,16384]{0,1:T(8,128)} %bitcast.127) | data formatting | bytes 7995392
  (42 shorter events, 1.4 us)
Async XLA Ops:
  7.2 101.4 %copy-start.3 = (f32[3,16384]{1,0:T(4,128)S(1)}, f32[3,16384]{1,0:T(4,128)}, u32[]{:S(2)}) copy-start(f32[3,16384]{1,0:T(4,128)} %param.11) | copy-start | bytes 589828
  7.2 102.1 %copy-start.4 = (f32[4,2,16384]{2,1,0:T(2,128)S(1)}, f32[4,2,16384]{2,1,0:T(2,128)}, u32[]{:S(2)}) copy-start(f32[4,2,16384]{2,1,0:T(2,128)} %param.14) | copy-start | bytes 1572868
  12.2 99.8 %all-to-all-start.1 = ((s32[32,1,1]{2,1,0:T(1,128)}), s32[32,1,1]{2,1,0:T(1,128)S(1)}, u32[]{:S(2)}, u32[]{:S(2)}) async-start(s32[32,1,1]{2,1,0:T(1,128)} %broadcast_in_dim.45), calls=%async_computation.1 | async-start | bytes 32768 | tf_op jit(solution)/shard_map/all_to_all | solution.py:11
  24.2 120.0 %copy-start.1 = (f32[3,16384]{1,0:T(4,128)S(1)}, f32[3,16384]{1,0:T(4,128)}, u32[]{:S(2)}) copy-start(f32[3,16384]{1,0:T(4,128)} %param.10) | copy-start | bytes 589828
  24.2 120.0 %copy-start.2 = (f32[4,16384]{1,0:T(4,128)S(1)}, f32[4,16384]{1,0:T(4,128)}, u32[]{:S(2)}) copy-start(f32[4,16384]{1,0:T(4,128)} %param.12) | copy-start | bytes 786436
  113.5 20.2 %all-to-all-start = ((f32[8,1,32768]{2,1,0:T(1,128)}), f32[8,1,32768]{2,1,0:T(1,128)S(1)}, u32[]{:S(2)}, u32[]{:S(2)}) async-start(f32[8,1,32768]{2,1,0:T(1,128)} %broadcast_in_dim.24), calls=%async_computation | async-start | bytes 2097152 | tf_op jit(solution)/shard_map/all_to_all | solution.py:11
  133.7 94.8 %all-to-all-start.2 = ((s32[1,32,4]{2,0,1:T(1,128)}), s32[1,32,4]{2,0,1:T(1,128)S(1)}, u32[]{:S(2)}, u32[]{:S(2)}) async-start(s32[1,32,4]{2,0,1:T(1,128)} %compare_select_fusion.1), calls=%async_computation.2 | async-start | bytes 32768 | tf_op jit(solution)/shard_map/all_to_all | solution.py:136
  228.5 21.8 %all-to-all-start.3 = ((f32[32,1,3904]{2,1,0:T(1,128)}), f32[32,1,3904]{2,1,0:T(1,128)S(1)}, u32[]{:S(2)}, u32[]{:S(2)}) async-start(f32[32,1,3904]{2,1,0:T(1,128)} %reshape.640), calls=%async_computation.3 | async-start | bytes 1015808 | tf_op jit(solution)/shard_map/all_to_all | solution.py:135
  237.6 74.3 %all-gather.2.cloned.1.call-start = ((), (), s32[]{:S(2)}) async-start(), calls=%async_computation.5 | async-start | bytes 9437184 | tf_op jit(solution)/shard_map/all_gather | solution.py:144
  258.8 1.0 copy-start
Sparse Core Ops, SparseCore 0:
  259.9 51.9 all-gather.1
where the time goes:
time: 329 us; the launch traced here: 327 us
  local copies, waits for them, and re-layouts  113 us (34%)
  other arithmetic  87.1 us (26%)
  waiting for transfers between devices  52.4 us (16%)
  starting transfers between devices  36.1 us (11%)
  between operations  21.3 us (6%)
  blocking collectives  16.9 us (5%)
    add x8, other arithmetic, view_stats(): first = [j00 * rot[0, j] + j02 * rot[2, j] for j in range(3)]  58.6 us
    scatter x1, local copies, waits for them, and re-layouts, body(): jnp.zeros((feat_rows, cap_blk * 128), jnp.float32).at[:, where_to]  44.3 us
    all_gather x1, waiting for transfers between devices, body(): placed = lax.all_gather(partial_place, 'view', axis=2, tiled=True)  32.5 us
    concatenate x2, local copies, waits for them, and re-layouts, body(): rows = jnp.concatenate([means, scales, quats, attrs, peak], axis=0)  28.5 us
    all_to_all x2, starting transfers between devices, copy_for_each(): lax.all_to_all(jnp.broadcast_to(x[None], (count, *x.shape)), axis, 0, 0,...  17.3 us
    all_to_all x1, blocking collectives, copy_for_each(): lax.all_to_all(jnp.broadcast_to(x[None], (count, *x.shape)), axis, 0, 0,...  16.9 us
    unnamed x15, local copies, waits for them, and re-layouts  11.7 us
    all_to_all x1, waiting for transfers between devices, body(): lax.all_to_all(portion, 'gauss', split_axis=1, concat_axis=1, tiled=True)  11.3 us
  transfers between devices with their start and end apart: 5, of which 3 were waited for; matrix products, arithmetic and copies ran while one was open for 54% of the time, Pallas kernels for 0%

commit v1 on v0

v1 whole, which is shorter than its diff:
```python
import functools

import jax
import jax.numpy as jnp
from jax import lax
from jax.experimental import pallas as pl
from jax.experimental.pallas import tpu as pltpu
from jax.sharding import PartitionSpec as P

G = 16384
ROWS = 61
BLK = 128
CAP = G // BLK
NV = 8
NG = 32
PER = CAP // NG
MESH = pl.DeviceIdType.MESH
VMEM = pl.BlockSpec(memory_space=pltpu.VMEM)
SMEM = pl.BlockSpec(memory_space=pltpu.SMEM)
ANY = pl.BlockSpec(memory_space=pl.ANY)


def stats_kernel(means, scales, quats, grad, seen, mask, rot, trans, focal, out, count):
    views = grad.shape[0]

    def step(c, _):
        s = pl.ds(pl.multiple_of(c * 1024, 1024), 1024)

        def row(ref, *at):
            return ref[at[:-1] + (slice(at[-1], at[-1] + 1), s)].reshape(8, 128)

        m = [row(means, i) for i in range(3)]
        sc = [row(scales, i) for i in range(3)]
        q = [row(quats, i) for i in range(4)]
        inv = 1.0 / jnp.sqrt(q[0] * q[0] + q[1] * q[1] + q[2] * q[2] + q[3] * q[3] + 0.25)
        w, x, y, z = (t * inv for t in q)
        rq = [
            [1 - 2 * (y * y + z * z), 2 * (x * y - w * z), 2 * (x * z + w * y)],
            [2 * (x * y + w * z), 1 - 2 * (x * x + z * z), 2 * (y * z - w * x)],
            [2 * (x * z - w * y), 2 * (y * z + w * x), 1 - 2 * (x * x + y * y)],
        ]
        factor = [[rq[i][j] * sc[j] for j in range(3)] for i in range(3)]
        gbest = jnp.zeros((8, 128), jnp.float32)
        lbest = jnp.zeros((8, 128), jnp.float32)
        for v in range(views):
            r = [[rot[v, i, j] for j in range(3)] for i in range(3)]
            p = [r[i][0] * m[0] + r[i][1] * m[1] + r[i][2] * m[2] + trans[v, i] for i in range(3)]
            near = 1.0 / jnp.maximum(p[2], 1.0)
            f = focal[v]
            j00 = f * near
            j02 = -j00 * p[0] * near
            j12 = -j00 * p[1] * near
            first = [j00 * r[0][j] + j02 * r[2][j] for j in range(3)]
            second = [j00 * r[1][j] + j12 * r[2][j] for j in range(3)]
            pr = [sum(first[j] * factor[j][k] for j in range(3)) for k in range(3)]
            qr = [sum(second[j] * factor[j][k] for j in range(3)) for k in range(3)]
            a = pr[0] * pr[0] + pr[1] * pr[1] + pr[2] * pr[2] + 0.3
            cc = qr[0] * qr[0] + qr[1] * qr[1] + qr[2] * qr[2] + 0.3
            b = pr[0] * qr[0] + pr[1] * qr[1] + pr[2] * qr[2]
            half = 0.5 * (a - cc)
            lam = 0.5 * (a + cc) + jnp.sqrt(half * half + b * b + 0.01)
            on = row(seen, v) > 0
            g0, g1 = row(grad, v, 0), row(grad, v, 1)
            gbest = jnp.maximum(gbest, jnp.where(on, g0 * g0 + g1 * g1, 0.0))
            lbest = jnp.maximum(lbest, jnp.where(on, lam, 0.0))
        part, at = c // 2, pl.multiple_of((c % 2) * 8, 8)
        out[part, 0, pl.ds(at, 8), :] = gbest
        out[part, 1, pl.ds(at, 8), :] = lbest
        return 0

    lax.fori_loop(0, 16, step, 0)
    columns = jnp.sum(mask[...].astype(jnp.float32), axis=0, keepdims=True)
    total = jnp.sum(columns, axis=1, keepdims=True)
    count[...] = jnp.broadcast_to(total, (8, 128)).astype(jnp.int32)


def peaks_kernel(part, count, best, counts, taken, merged, s1, r1, s2, r2, s3, r3):
    v, g = lax.axis_index("view"), lax.axis_index("gauss")
    barrier = pltpu.get_barrier_semaphore()

    def hello_v(i, _):
        pl.semaphore_signal(barrier, inc=1, device_id={"view": (v + i) % NV}, device_id_type=MESH)
        return 0

    def hello_g(i, _):
        pl.semaphore_signal(barrier, inc=1, device_id={"gauss": (g + i) % NG}, device_id_type=MESH)
        return 0

    lax.fori_loop(1, NV, hello_v, 0)
    lax.fori_loop(1, NG, hello_g, 0)
    pl.semaphore_wait(barrier, NV - 1 + NG - 1)

    def scatter(i, slot):
        peer = (v + i) % NV
        return pltpu.make_async_remote_copy(
            part.at[peer], taken.at[slot], s1.at[i], r1.at[slot], device_id={"view": peer}, device_id_type=MESH
        )

    def spread(i, slot):
        peer = (v + i) % NV
        return pltpu.make_async_remote_copy(
            merged, best.at[slot], s2.at[i], r2.at[slot], device_id={"view": peer}, device_id_type=MESH
        )

    def tell(i, slot):
        peer = (g + i) % NG
        return pltpu.make_async_remote_copy(
            count, counts.at[slot], s3.at[i], r3.at[slot], device_id={"gauss": peer}, device_id_type=MESH
        )

    def each(n, do):
        def one(i, _):
            do(i)
            return 0

        lax.fori_loop(1, n, one, 0)

    each(NV, lambda i: scatter(i, v).start())
    each(NG, lambda i: tell(i, g).start())
    counts[g] = count[...]
    each(NV, lambda i: scatter(i, (v + i) % NV).wait_recv())

    top = part[v]

    def merge(i, top):
        return jnp.maximum(top, taken[(v + i) % NV])

    top = lax.fori_loop(1, NV, merge, top)
    merged[...] = top
    best[v] = top
    each(NV, lambda i: spread(i, v).start())
    each(NV, lambda i: spread(i, (v + i) % NV).wait_recv())
    each(NG, lambda i: tell(i, (g + i) % NG).wait_recv())
    each(NV, lambda i: scatter(i, v).wait_send())
    each(NV, lambda i: spread(i, v).wait_send())
    each(NG, lambda i: tell(i, g).wait_send())


def pack_kernel(mask, counts, best, means, scales, quats, attrs, out, table, peak, xa, xb, x, picks, tab, stab, sem):
    v, g = lax.axis_index("view"), lax.axis_index("gauss")
    a_at = pl.multiple_of(jnp.clip(v - 2, 0, 5) * 8, 8)
    b_at = pl.multiple_of(jnp.clip(v - 1, 0, 5) * 8, 8)
    load_a = pltpu.make_async_copy(attrs.at[pl.ds(a_at, 8), :], xa, sem.at[0])
    load_b = pltpu.make_async_copy(attrs.at[pl.ds(b_at, 8), :], xb, sem.at[1])
    load_c = pltpu.make_async_copy(attrs.at[48:49, :], xb.at[0:1, :], sem.at[1])
    load_a.start()

    @pl.when(v < 7)
    def _():
        load_b.start()

    @pl.when(v == 7)
    def _():
        load_c.start()

    sub = lax.broadcasted_iota(jnp.int32, (8, 128), 0)
    lane = lax.broadcasted_iota(jnp.int32, (8, 128), 1)
    k = lane * NG + g
    off = jnp.zeros((8, 128), jnp.int32)
    mine = jnp.zeros((8, 128), jnp.int32)
    total = jnp.zeros((8, 128), jnp.int32)
    source = jnp.full((8, 128), CAP, jnp.int32)
    for s in range(NG):
        n = counts[s]
        blocks = (n + (BLK - 1)) >> 7
        mine = mine + jnp.where(s < g, blocks, 0)
        inside = (k >= off) & (k < off + blocks)
        source = jnp.where(inside, s * PER + ((k - off) >> 5), source)
        off = off + blocks
        total = total + n
    slots = (off + (NG - 1)) >> 5
    table[...] = jnp.where(sub == 0, source, jnp.where(sub == 1, total, slots))

    marks = mask[...].astype(jnp.float32).astype(jnp.bfloat16)
    i0 = lax.broadcasted_iota(jnp.int32, (128, 128), 0)
    i1 = lax.broadcasted_iota(jnp.int32, (128, 128), 1)
    upto = (i0 <= i1).astype(jnp.float32).astype(jnp.bfloat16)
    before = (i0 < i1).astype(jnp.float32).astype(jnp.bfloat16)
    run = jnp.dot(marks, upto, preferred_element_type=jnp.float32).astype(jnp.int32)
    per_row = lax.dot_general(
        jnp.ones((8, 128), jnp.bfloat16), marks, (((1,), (1,)), ((), ())), preferred_element_type=jnp.float32
    )
    base = jnp.dot(per_row.astype(jnp.bfloat16), before, preferred_element_type=jnp.float32)
    end = (base + per_row).astype(jnp.int32)
    tab[...] = jnp.where(sub == 0, base.astype(jnp.int32), jnp.where(sub == 1, end, mine))
    to_smem = pltpu.make_async_copy(tab, stab, sem.at[2])
    to_smem.start()

    e = jnp.where(mask[...] > 0, i1 + ((i1 - run + 1) << 8), 0)
    for bit in range(7):
        far = pltpu.roll(e, 128 - (1 << bit), axis=1)
        comes = (far & (256 << bit)) != 0
        goes = (e & (256 << bit)) != 0
        e = jnp.where(comes, far, jnp.where(goes, 0, e))
    picks[...] = e & 255

    def roots(c, _):
        s = pl.ds(pl.multiple_of(c * 1024, 1024), 1024)
        part, at = c // 2, pl.multiple_of((c % 2) * 8, 8)
        peak[0:1, s] = jnp.sqrt(best[part, 0, pl.ds(at, 8), :]).reshape(1, 1024)
        peak[1:2, s] = (3.0 * jnp.sqrt(best[part, 1, pl.ds(at, 8), :])).reshape(1, 1024)
        return 0

    lax.fori_loop(0, 16, roots, 0)

    load_a.wait()

    @pl.when(v < 7)
    def _():
        load_b.wait()

    @pl.when(v == 7)
    def _():
        load_c.wait()

    @pl.when(v == 0)
    def _():
        x[0:3, :] = means[...]
        x[3:6, :] = scales[...]
        x[6:8, :] = quats[0:2, :]

    @pl.when(v == 1)
    def _():
        x[0:2, :] = quats[2:4, :]
        x[2:8, :] = xb[0:6, :]

    @pl.when((v > 1) & (v < 7))
    def _():
        x[0:2, :] = xa[6:8, :]
        x[2:8, :] = xb[0:6, :]

    @pl.when(v == 7)
    def _():
        x[0:2, :] = xa[6:8, :]
        x[2:3, :] = xb[0:1, :]
        x[3:5, :] = peak[...]
        x[5:8, :] = jnp.zeros((3, G), jnp.float32)

    to_smem.wait()
    shift = stab[2, 0]

    def home(block):
        return ((shift + block) & (NG - 1)) * PER + (block >> 5)

    def pack(c, carry):
        start, stop = stab[0, c], stab[1, c]
        block, r = start >> 7, start & 127
        tile = x[:, pl.ds(pl.multiple_of(c * 128, 128), 128)]
        pick = jnp.broadcast_to(picks[pl.ds(c, 1), :], (8, 128))
        got = jnp.take_along_axis(tile, pick, axis=1, mode="promise_in_bounds")
        got = pltpu.roll(got, r, axis=1)
        live = ((lane - r) & 127) < (stop - start)
        now = jnp.where(live & (lane >= r), got, carry)
        later = jnp.where(live & (lane < r), got, 0.0)
        out[home(block)] = now
        return jnp.where((stop >> 7) > block, later, now)

    carry = lax.fori_loop(0, 128, pack, jnp.zeros((8, 128), jnp.float32), unroll=4)
    last = stab[1, 127]

    @pl.when(last < G)
    def _():
        out[home(last >> 7)] = carry


def move_kernel(tiles, table, out, taken, placed, s1, r1, s2, r2, s3, r3, own):
    v, g = lax.axis_index("view"), lax.axis_index("gauss")
    core, chip = v % 2, v // 2
    barrier = pltpu.get_barrier_semaphore()

    def each(lo, n, do):
        def one(i, _):
            do(i)
            return 0

        lax.fori_loop(lo, n, one, 0)

    each(1, NV, lambda i: pl.semaphore_signal(barrier, inc=1, device_id={"view": (v + i) % NV}, device_id_type=MESH))
    each(1, NG, lambda i: pl.semaphore_signal(barrier, inc=1, device_id={"gauss": (g + i) % NG}, device_id_type=MESH))
    pl.semaphore_wait(barrier, NV - 1 + NG - 1)

    def send(i, slot):
        peer = (g + i) % NG
        return pltpu.make_async_remote_copy(
            tiles.at[pl.ds(peer * PER, PER)],
            taken.at[pl.ds(slot * PER, PER)],
            s1.at[i],
            r1.at[slot],
            device_id={"gauss": peer},
            device_id_type=MESH,
        )

    each(1, NG, lambda i: send(i, g).start())
    keep = pltpu.make_async_copy(tiles.at[pl.ds(g * PER, PER)], taken.at[pl.ds(g * PER, PER)], own.at[0])
    keep.start()
    taken[CAP] = jnp.zeros((8, 128), jnp.float32)
    keep.wait()
    each(1, NG, lambda i: send(i, (g + i) % NG).wait_recv())

    def place(q, _):
        placed[q] = taken[table[0, q]]
        return 0

    lax.fori_loop(0, CAP, place, 0)

    def away(i, slot):
        peer = ((chip + i) % 4) * 2 + core
        return pltpu.make_async_remote_copy(
            placed, out.at[slot], s2.at[i], r2.at[slot], device_id={"view": peer}, device_id_type=MESH
        )

    def beside(i, slot):
        src = placed if i is None else out.at[slot]
        at = 0 if i is None else i
        return pltpu.make_async_remote_copy(
            src, out.at[slot], s3.at[at], r3.at[slot], device_id={"view": chip * 2 + 1 - core}, device_id_type=MESH
        )

    each(1, 4, lambda i: away(i, v).start())
    beside(None, v).start()
    mine = pltpu.make_async_copy(placed, out.at[v], own.at[0])
    mine.start()

    def relay(i):
        slot = ((chip + i) % 4) * 2 + core
        away(i, slot).wait_recv()
        beside(i, slot).start()

    each(1, 4, relay)
    mine.wait()
    beside(None, chip * 2 + 1 - core).wait_recv()
    each(1, 4, lambda i: beside(i, ((chip + i) % 4) * 2 + 1 - core).wait_recv())
    each(1, 4, lambda i: away(i, v).wait_send())
    beside(None, v).wait_send()
    each(1, 4, lambda i: beside(i, ((chip + i) % 4) * 2 + core).wait_send())
    each(1, NG, lambda i: send(i, g).wait_send())


HALF = 64


def lay_kernel(slots, tiles, out):
    h = pl.program_id(1)
    for q in range(HALF):
        out[:, q * BLK : (q + 1) * BLK] = jnp.where(h * HALF + q < slots[0], tiles[0, q], 0.0)


def body(means, scales, quats, attrs, grad_screen, visible, clone_mask, rotation, shift, focal):
    f32, i32 = jnp.float32, jnp.int32
    mask = clone_mask.reshape(128, 128)
    part, count = pl.pallas_call(
        stats_kernel,
        in_specs=[VMEM] * 6 + [SMEM] * 3,
        out_specs=(VMEM, VMEM),
        out_shape=(jax.ShapeDtypeStruct((NV, 2, 16, 128), f32), jax.ShapeDtypeStruct((8, 128), i32)),
        name="stats",
    )(means, scales, quats, grad_screen, visible, mask, rotation, shift, focal)

    dma = pltpu.SemaphoreType.DMA
    best, counts = pl.pallas_call(
        peaks_kernel,
        in_specs=[VMEM] * 2,
        out_specs=(VMEM, VMEM),
        out_shape=(jax.ShapeDtypeStruct((NV, 2, 16, 128), f32), jax.ShapeDtypeStruct((NG, 8, 128), i32)),
        scratch_shapes=[
            pltpu.VMEM((NV, 2, 16, 128), f32),
            pltpu.VMEM((2, 16, 128), f32),
            dma((NV,)),
            dma((NV,)),
            dma((NV,)),
            dma((NV,)),
            dma((NG,)),
            dma((NG,)),
        ],
        compiler_params=pltpu.CompilerParams(collective_id=0, has_side_effects=True),
        name="peaks",
    )(part, count)

    tiles, table, peak = pl.pallas_call(
        pack_kernel,
        in_specs=[VMEM] * 6 + [ANY],
        out_specs=(VMEM, VMEM, VMEM),
        out_shape=(
            jax.ShapeDtypeStruct((CAP, 8, 128), f32),
            jax.ShapeDtypeStruct((8, 128), i32),
            jax.ShapeDtypeStruct((2, G), f32),
        ),
        scratch_shapes=[
            pltpu.VMEM((8, G), f32),
            pltpu.VMEM((8, G), f32),
            pltpu.VMEM((8, G), f32),
            pltpu.VMEM((128, 128), i32),
            pltpu.VMEM((8, 128), i32),
            pltpu.SMEM((8, 128), i32),
            dma((3,)),
        ],
        name="pack",
    )(mask, counts, best, means, scales, quats, attrs)

    gathered = pl.pallas_call(
        move_kernel,
        in_specs=[VMEM, SMEM],
        out_specs=ANY,
        out_shape=jax.ShapeDtypeStruct((NV, CAP, 8, 128), f32),
        scratch_shapes=[
            pltpu.VMEM((CAP + 1, 8, 128), f32),
            pltpu.VMEM((CAP, 8, 128), f32),
            dma((NG,)),
            dma((NG,)),
            dma((4,)),
            dma((NV,)),
            dma((4,)),
            dma((NV,)),
            dma((1,)),
        ],
        compiler_params=pltpu.CompilerParams(collective_id=1, has_side_effects=True),
        name="move",
    )(tiles, table)

    slots = table[2, :1]
    clones = pl.pallas_call(
        lay_kernel,
        grid_spec=pltpu.PrefetchScalarGridSpec(
            num_scalar_prefetch=1,
            grid=(NV, CAP // HALF),
            in_specs=[
                pl.BlockSpec(
                    (1, HALF, 8, 128), lambda r, h, n: (r, jnp.minimum(h, (jnp.maximum(n[0], 1) - 1) // HALF), 0, 0)
                )
            ],
            out_specs=pl.BlockSpec((8, HALF * BLK), lambda r, h, n: (r, h)),
        ),
        out_shape=jax.ShapeDtypeStruct((ROWS, G), f32),
        name="lay",
    )(slots, gathered)
    return (peak, clones, table[1, 0])


def solution(mesh):
    return jax.shard_map(
        body,
        mesh=mesh,
        in_specs=(
            P(None, "gauss"),
            P(None, "gauss"),
            P(None, "gauss"),
            P(None, "gauss"),
            P("view", None, "gauss"),
            P("view", "gauss"),
            P("gauss"),
            P("view", None, None),
            P("view", None),
            P("view"),
        ),
        out_specs=(P(None, "gauss"), P(None, "gauss"), P()),
        check_vma=False,
    )
```

time: 329 us -> 98.5 us (0.30)
  local copies, waits for them, and re-layouts: 113 us -> 2.63 us
  Pallas kernels: 0 us -> 94.7 us
  other arithmetic: 87.1 us -> 0 us
  waiting for transfers between devices: 52.4 us -> 0 us
  starting transfers between devices: 36.1 us -> 0 us
  between operations: 21.3 us -> 0.66 us
  blocking collectives: 16.9 us -> 0 us
    pallas_call x0 -> x5, Pallas kernels: none -> 94.7 us  [the longest x1 48.7 us: body(): pl.pallas_call(move_kernel, in_specs=[VMEM, SMEM], out_specs=ANY, out_sha...]
    add x16 -> x0, other arithmetic: 68.8 us -> none  [the longest x8 58.6 us: view_stats(): first = [j00 * rot[0, j] + j02 * rot[2, j] for j in range(3)]]
    scatter x2 -> x0, local copies, waits for them, and re-layouts: 48.9 us -> none  [the longest x1 44.3 us: body(): jnp.zeros((feat_rows, cap_blk * 128), jnp.float32).at[:, where_to]]
    all_to_all x4 -> x0, starting transfers between devices: 36 us -> none  [the longest x2 17.3 us: copy_for_each(): lax.all_to_all(jnp.broadcast_to(x[None], (count, *x.shape)), axis, 0, 0,...]
    all_gather x1 -> x0, waiting for transfers between devices: 32.5 us -> none  [body(): placed = lax.all_gather(partial_place, 'view', axis=2, tiled=True)]
    concatenate x2 -> x0, local copies, waits for them, and re-layouts: 28.5 us -> none  [body(): rows = jnp.concatenate([means, scales, quats, attrs, peak], axis=0)]
    all_to_all x4 -> x0, waiting for transfers between devices: 19.8 us -> none  [the longest x1 11.3 us: body(): lax.all_to_all(portion, 'gauss', split_axis=1, concat_axis=1, tiled=True)]
    all_to_all x1 -> x0, blocking collectives: 16.9 us -> none  [copy_for_each(): lax.all_to_all(jnp.broadcast_to(x[None], (count, *x.shape)), axis, 0, 0,...]
  transfers between devices with their start and end apart: 5 -> 0, of which waited for: 3 -> 0; matrix products, arithmetic and copies ran while one was open for 54% -> 0% of each run, Pallas kernels for 0% -> 0%
where the time goes in v1:
time: 98.5 us; the launch traced here: 98 us
  Pallas kernels  94.7 us (96%)
  local copies, waits for them, and re-layouts  2.63 us (3%)
    pallas_call x1, Pallas kernels, body(): pl.pallas_call(move_kernel, in_specs=[VMEM, SMEM], out_specs=ANY, out_sha...  48.7 us
    pallas_call x1, Pallas kernels, body(): pl.pallas_call(peaks_kernel, in_specs=[VMEM] * 2, out_specs=(VMEM, VMEM),...  22.8 us
    pallas_call x1, Pallas kernels, body(): pl.pallas_call(lay_kernel, grid_spec=pltpu.PrefetchScalarGridSpec(num_sca...  11.1 us
    pallas_call x1, Pallas kernels, body(): pl.pallas_call(pack_kernel, in_specs=[VMEM] * 6 + [ANY], out_specs=(VMEM,...  8.66 us
    pallas_call x1, Pallas kernels, body(): pl.pallas_call(stats_kernel, in_specs=[VMEM] * 6 + [SMEM] * 3, out_specs=...  3.56 us

profile of v1, /device:TPU:1, one launch (start us, length us, event | category | flops | bytes accessed | tf_op | source)
XLA Modules:
  0.0 98.0 jit_solution(5991776020686121531)
XLA Ops:
  0.6 1.3 %copy.13.rot = f32[4,3,3]{2,1,0:T(4,128)} copy(f32[4,3,3]{2,0,1:T(4,128)} %param.17) | data formatting | bytes 288 | tf_op args[7]
  1.9 3.6 %stats.1 = (f32[8,2,16,128]{3,2,1,0:T(8,128)}, s32[8,128]{1,0:T(8,128)}) custom-call(f32[3,16384]{1,0:T(4,128)} %means.3, f32[3,16384]{1,0:T(4,128)} %scales.3, f32[4,16384]{1,0:T(4,128)} %quats.3, f32[4,2,16384]{2,1,0:T(2,128)} %grad.1, s32[4,16384]{1,0:T(4,128)} %seen.1, s32[128,128]{1,0:T(8,128)} %bitcast.3, f32[4,3,3]{2,1,0:T(4,128)} %copy.13.rot, ...), custom_call_target="tpu_custom_call" | custom-call | tf_op jit(solution)/shard_map/stats/pallas_call | solution.py:351
  5.5 22.8 %peaks.1 = (f32[8,2,16,128]{3,2,1,0:T(8,128)}, s32[32,8,128]{2,1,0:T(8,128)}) custom-call(f32[8,2,16,128]{3,2,1,0:T(8,128)} %get-tuple-element.10.part, s32[8,128]{1,0:T(8,128)} %get-tuple-element.11.count), custom_call_target="tpu_custom_call" | custom-call | tf_op jit(solution)/shard_map/peaks/pallas_call | solution.py:360
  28.3 8.7 %pack.1 = (f32[128,8,128]{2,1,0:T(8,128)}, s32[8,128]{1,0:T(8,128)}, f32[2,16384]{1,0:T(2,128)}) custom-call(s32[128,128]{1,0:T(8,128)} %bitcast.4, s32[32,8,128]{2,1,0:T(8,128)} %get-tuple-element.12.counts, f32[8,2,16,128]{3,2,1,0:T(8,128)} %get-tuple-element.13.best, f32[3,16384]{1,0:T(4,128)} %means.3, f32[3,16384]{1,0:T(4,128)} %scales.3, ...), custom_call_target="tpu_custom_call" | custom-call | tf_op jit(solution)/shard_map/pack/pallas_call | solution.py:379
  36.9 1.3 %fusion = (s32[1,1]{1,0:T(1,128)}, s32[1,1]{1,0:T(1,128)}) fusion(s32[8,128]{1,0:T(8,128)} %get-tuple-element.15.table), kind=kLoop, calls=%fused_computation | loop fusion | bytes 16 | tf_op jit(solution)/shard_map/slice | solution.py:436
  38.3 48.7 %move.1.tiles = f32[8,128,8,128]{3,2,1,0:T(8,128)} custom-call(f32[128,8,128]{2,1,0:T(8,128)} %get-tuple-element.16.tiles, s32[8,128]{1,0:T(8,128)} %get-tuple-element.15.table), custom_call_target="tpu_custom_call" | custom-call | tf_op jit(solution)/shard_map/move/pallas_call | solution.py:400
  86.9 11.1 %lay.1 = f32[61,16384]{1,0:T(8,128)} custom-call(s32[1]{0:T(128)} %bitcast.1.slots, f32[8,128,8,128]{3,2,1,0:T(8,128)} %move.1.tiles), custom_call_target="tpu_custom_call" | custom-call | tf_op jit(solution)/shard_map/lay/pallas_call | solution.py:421

commit v2 on v0

v2 whole, which is shorter than its diff:
```python
import jax
import jax.numpy as jnp
from jax import lax
from jax.experimental import pallas as pl
from jax.experimental.pallas import tpu as pltpu
from jax.sharding import PartitionSpec as P

G = 16384
ROWS = 61
BLK = 128
CAP = G // BLK
NV = 8
NG = 32
PER = CAP // NG
PAIR = PER * BLK
CHUNKS = 8
WIDE = G // CHUNKS
MESH = pl.DeviceIdType.MESH
VMEM = pl.BlockSpec(memory_space=pltpu.VMEM)
SMEM = pl.BlockSpec(memory_space=pltpu.SMEM)
ANY = pl.BlockSpec(memory_space=pl.ANY)


def each(lo, n, do):
    def one(i, _):
        do(i)
        return 0

    lax.fori_loop(lo, n, one, 0)


def front_kernel(
    mask, means, scales, quats, grad, seen, rot, trans, focal, attrs,
    part, packed, tiles, count,
    xa, xb, x, gl, picks, tab, stab, sem,
):
    v = lax.axis_index("view")
    a_at = pl.multiple_of(jnp.clip(v - 2, 0, 5) * 8, 8)
    b_at = pl.multiple_of(jnp.clip(v - 1, 0, 5) * 8, 8)
    load_a = pltpu.make_async_copy(attrs.at[pl.ds(a_at, 8), :], xa, sem.at[0])
    load_b = pltpu.make_async_copy(attrs.at[pl.ds(b_at, 8), :], xb, sem.at[1])
    load_c = pltpu.make_async_copy(attrs.at[48:49, :], xb.at[0:1, :], sem.at[1])
    load_a.start()

    @pl.when(v < 7)
    def _():
        load_b.start()

    @pl.when(v == 7)
    def _():
        load_c.start()

    sub = lax.broadcasted_iota(jnp.int32, (8, 128), 0)
    lane = lax.broadcasted_iota(jnp.int32, (8, 128), 1)
    marks = mask[...].astype(jnp.float32).astype(jnp.bfloat16)
    i0 = lax.broadcasted_iota(jnp.int32, (128, 128), 0)
    i1 = lax.broadcasted_iota(jnp.int32, (128, 128), 1)
    upto = (i0 <= i1).astype(jnp.float32).astype(jnp.bfloat16)
    before = (i0 < i1).astype(jnp.float32).astype(jnp.bfloat16)
    after = (i0 > i1).astype(jnp.float32).astype(jnp.bfloat16)
    run = jnp.dot(marks, upto, preferred_element_type=jnp.float32).astype(jnp.int32)
    in_lanes = lax.dot_general(
        jnp.ones((8, 128), jnp.bfloat16), marks, (((1,), (1,)), ((), ())), preferred_element_type=jnp.float32
    )
    base = jnp.dot(in_lanes.astype(jnp.bfloat16), before, preferred_element_type=jnp.float32)
    end = base + in_lanes
    tab[...] = jnp.where(sub == 0, base, end).astype(jnp.int32)
    to_smem = pltpu.make_async_copy(tab, stab, sem.at[2])
    to_smem.start()
    total = jnp.sum(in_lanes, axis=1, keepdims=True)
    count[...] = jnp.broadcast_to(total, (8, 128)).astype(jnp.int32)

    in_row = jnp.dot(marks, jnp.ones((128, 128), jnp.bfloat16), preferred_element_type=jnp.float32)
    row_base = jnp.dot(after, in_row.astype(jnp.bfloat16), preferred_element_type=jnp.float32).astype(jnp.int32)
    e = jnp.where(mask[...] > 0, i1 + 128 + ((i1 - run + 1) << 8), 0)
    for bit in range(7):
        far = pltpu.roll(e, 128 - (1 << bit), axis=1)
        comes = (far & (256 << bit)) != 0
        goes = (e & (256 << bit)) != 0
        e = jnp.where(comes, far, jnp.where(goes, 0, e))
    e = e & 255
    turn = row_base & 127
    for bit in range(7):
        e = jnp.where((turn & (1 << bit)) != 0, pltpu.roll(e, 1 << bit, axis=1), e)
    picks[...] = e | jnp.where(i1 < turn, 256, 0)

    def step(c, _):
        s = pl.ds(pl.multiple_of(c * 1024, 1024), 1024)

        def row(ref, *at):
            return ref[at[:-1] + (slice(at[-1], at[-1] + 1), s)].reshape(8, 128)

        m = [row(means, i) for i in range(3)]
        sc = [row(scales, i) for i in range(3)]
        q = [row(quats, i) for i in range(4)]
        inv = 1.0 / jnp.sqrt(q[0] * q[0] + q[1] * q[1] + q[2] * q[2] + q[3] * q[3] + 0.25)
        w, xq, y, z = (t * inv for t in q)
        rq = [
            [1 - 2 * (y * y + z * z), 2 * (xq * y - w * z), 2 * (xq * z + w * y)],
            [2 * (xq * y + w * z), 1 - 2 * (xq * xq + z * z), 2 * (y * z - w * xq)],
            [2 * (xq * z - w * y), 2 * (y * z + w * xq), 1 - 2 * (xq * xq + y * y)],
        ]
        factor = [[rq[i][j] * sc[j] for j in range(3)] for i in range(3)]
        gbest = jnp.zeros((8, 128), jnp.float32)
        lbest = jnp.zeros((8, 128), jnp.float32)
        for n in range(seen.shape[0]):
            r = [[rot[i, n, j] for j in range(3)] for i in range(3)]
            p = [r[i][0] * m[0] + r[i][1] * m[1] + r[i][2] * m[2] + trans[n, i] for i in range(3)]
            near = 1.0 / jnp.maximum(p[2], 1.0)
            j00 = focal[n] * near
            j02 = -j00 * p[0] * near
            j12 = -j00 * p[1] * near
            first = [j00 * r[0][j] + j02 * r[2][j] for j in range(3)]
            second = [j00 * r[1][j] + j12 * r[2][j] for j in range(3)]
            pr = [sum(first[j] * factor[j][k] for j in range(3)) for k in range(3)]
            qr = [sum(second[j] * factor[j][k] for j in range(3)) for k in range(3)]
            a = pr[0] * pr[0] + pr[1] * pr[1] + pr[2] * pr[2] + 0.3
            cc = qr[0] * qr[0] + qr[1] * qr[1] + qr[2] * qr[2] + 0.3
            b = pr[0] * qr[0] + pr[1] * qr[1] + pr[2] * qr[2]
            half = 0.5 * (a - cc)
            lam = 0.5 * (a + cc) + jnp.sqrt(half * half + b * b + 0.01)
            on = row(seen, n) > 0
            g0, g1 = row(grad, n, 0), row(grad, n, 1)
            gbest = jnp.maximum(gbest, jnp.where(on, g0 * g0 + g1 * g1, 0.0))
            lbest = jnp.maximum(lbest, jnp.where(on, lam, 0.0))
        piece, at = c // 2, pl.multiple_of((c % 2) * 8, 8)
        part[piece, 0, pl.ds(at, 8), :] = gbest
        part[piece, 1, pl.ds(at, 8), :] = lbest
        gl[0:1, s] = gbest.reshape(1, 1024)
        gl[1:2, s] = lbest.reshape(1, 1024)
        return 0

    lax.fori_loop(0, 16, step, 0)

    load_a.wait()

    @pl.when(v < 7)
    def _():
        load_b.wait()

    @pl.when(v == 7)
    def _():
        load_c.wait()

    @pl.when(v == 0)
    def _():
        x[0:3, :] = means[...]
        x[3:6, :] = scales[...]
        x[6:8, :] = quats[0:2, :]

    @pl.when(v == 1)
    def _():
        x[0:2, :] = quats[2:4, :]
        x[2:8, :] = xb[0:6, :]

    @pl.when((v > 1) & (v < 7))
    def _():
        x[0:2, :] = xa[6:8, :]
        x[2:8, :] = xb[0:6, :]

    @pl.when(v == 7)
    def _():
        x[0:2, :] = xa[6:8, :]
        x[2:3, :] = xb[0:1, :]
        x[3:8, :] = jnp.zeros((5, G), jnp.float32)

    to_smem.wait()

    def pack(c, carry):
        block = stab[0, c] >> 7
        full = (stab[1, c] >> 7) > block
        cols = pl.ds(pl.multiple_of(c * 128, 128), 128)
        pick = jnp.broadcast_to(picks[pl.ds(c, 1), :], (8, 128))
        at, kind = pick & 127, pick & 384
        here, later = kind == 128, kind == 384
        done = []
        for ref, old in zip((x, gl), carry):
            got = jnp.take_along_axis(ref[:, cols], at, axis=1, mode="promise_in_bounds")
            now = jnp.where(here, got, old)
            done.append((now, jnp.where(full, jnp.where(later, got, 0.0), now)))
        tiles[block] = done[0][0]
        packed[block] = done[1][0][0:2]
        return done[0][1], done[1][1]

    zero = jnp.zeros((8, 128), jnp.float32)
    left = lax.fori_loop(0, 128, pack, (zero, zero), unroll=8)
    last = stab[1, 127]

    @pl.when(last < G)
    def _():
        tiles[last >> 7] = left[0]
        packed[last >> 7] = left[1][0:2]


def move_kernel(
    part, packed, tiles, count,
    out, best, counts,
    taken, takenp, merged, mergedp, allp, turned, tab, stab,
    s_part, r_part, s_pack, r_pack, s_best, r_best, s_all, r_all, s_count, r_count, s_pair, r_pair,
    s_own, r_own, s_side, r_side, s_far, r_far, own,
):
    v, g = lax.axis_index("view"), lax.axis_index("gauss")
    core, chip = v % 2, v // 2
    gy, gz = g // 8, g % 8
    barrier = pltpu.get_barrier_semaphore()
    each(1, NV, lambda i: pl.semaphore_signal(barrier, inc=1, device_id={"view": (v + i) % NV}, device_id_type=MESH))
    each(1, NG, lambda i: pl.semaphore_signal(barrier, inc=1, device_id={"gauss": (g + i) % NG}, device_id_type=MESH))
    pl.semaphore_wait(barrier, NV - 1 + NG - 1)

    def over_view(peer, src, dst, s, r):
        return pltpu.make_async_remote_copy(src, dst, s, r, device_id={"view": peer}, device_id_type=MESH)

    def over_gauss(peer, src, dst, s, r):
        return pltpu.make_async_remote_copy(src, dst, s, r, device_id={"gauss": peer}, device_id_type=MESH)

    def tell(i, slot):
        return over_gauss((g + i) % NG, count, counts.at[slot], s_count.at[i], r_count.at[slot])

    def give_part(i, slot):
        peer = (v + i) % NV
        return over_view(peer, part.at[peer], taken.at[slot], s_part.at[i], r_part.at[slot])

    def give_pack(i, slot):
        peer = (v + i) % NV
        src = packed.at[pl.ds(peer * 16, 16)]
        return over_view(peer, src, takenp.at[slot], s_pack.at[i], r_pack.at[slot])

    def give_best(i, slot):
        return over_view((v + i) % NV, merged, best.at[slot], s_best.at[i], r_best.at[slot])

    def give_all(slot):
        return over_view(NV - 1, mergedp, allp.at[pl.ds(slot * 16, 16)], s_all.at[0], r_all.at[slot])

    each(1, NG, lambda i: tell(i, g).start())
    each(1, NV, lambda i: give_pack(i, v).start())
    each(1, NV, lambda i: give_part(i, v).start())
    counts[g] = count[...]
    each(1, NG, lambda i: tell(i, (g + i) % NG).wait_recv())

    def add(s, mine):
        return mine + jnp.where(s < g, (counts[s] + (BLK - 1)) >> 7, 0)

    tab[...] = lax.fori_loop(0, NG, add, jnp.zeros((8, 128), jnp.int32))
    to_smem = pltpu.make_async_copy(tab, stab, own.at[0])
    to_smem.start()
    to_smem.wait()
    shift = stab[0, 0]

    rows = pl.ds(pl.multiple_of(v * 8, 8), 8)

    def span(at, size):
        return pl.ds(pl.multiple_of(at * size, size), size)

    def owner(i):
        return ((gy + i // 8) % 4) * 8 + (gz + i % 8) % 8

    def pair(i):
        return over_gauss(owner(i), turned.at[:, span(i, PAIR)], out.at[rows, span(i, PAIR)], s_pair.at[i], r_pair.at[i])

    keep = pltpu.make_async_copy(turned.at[:, 0:PAIR], out.at[rows, 0:PAIR], own.at[1])

    def turn(finish):
        def one(i, _):
            block = (owner(i) - shift) & (NG - 1)
            for w in range(PER):
                tile = finish(tiles[block + w * NG], block + w * NG)
                turned[:, span(i * PER + w, BLK)] = tile
            return 0

        lax.fori_loop(0, NG, one, 0)
        each(1, NG, lambda i: pair(i).start())
        keep.start()

    @pl.when(v < NV - 1)
    def _():
        turn(lambda tile, block: tile)

    each(1, NV, lambda i: give_pack(i, (v + i) % NV).wait_recv())

    def merge_p(i, top):
        return jnp.maximum(top, takenp[(v + i) % NV])

    topp = lax.fori_loop(1, NV, merge_p, packed[pl.ds(v * 16, 16)])
    mergedp[...] = topp

    @pl.when(v < NV - 1)
    def _():
        give_all(v).start()

    @pl.when(v == NV - 1)
    def _():
        allp[pl.ds(v * 16, 16)] = topp

    each(1, NV, lambda i: give_part(i, (v + i) % NV).wait_recv())

    def merge(i, top):
        return jnp.maximum(top, taken[(v + i) % NV])

    top = lax.fori_loop(1, NV, merge, part[v])
    merged[...] = top
    best[v] = top
    each(1, NV, lambda i: give_best(i, v).start())

    @pl.when(v == NV - 1)
    def _():
        each(0, NV - 1, lambda i: give_all(i).wait_recv())
        sub = lax.broadcasted_iota(jnp.int32, (8, 128), 0)

        def finish(tile, block):
            pair_rows = allp[block]
            gtop = jnp.broadcast_to(jnp.sqrt(pair_rows[0:1]), (8, 128))
            ltop = jnp.broadcast_to(3.0 * jnp.sqrt(pair_rows[1:2]), (8, 128))
            return jnp.where(sub == 3, gtop, jnp.where(sub == 4, ltop, tile))

        turn(finish)

    mate = chip * 2 + 1 - core
    right, left, far = (((chip + i) % 4) * 2 + core for i in (1, 3, 2))

    def cut(group, c):
        at = out.at[pl.ds(pl.multiple_of(group * 8, 8), 8), span(c, WIDE)]
        return at, at

    def side(kind, c, group):
        return over_view(mate, *cut(group, c), s_side.at[kind, c], r_side.at[kind, c])

    def go(way, c, group):
        peer = right if way == 0 else left
        return over_view(peer, *cut(group, c), s_own.at[way, c], r_own.at[way, c])

    def on(way, c, group):
        peer = right if way == 0 else left
        return over_view(peer, *cut(group, c), s_far.at[c], r_far.at[c])

    def a_step(c):
        @pl.when(c == 0)
        def _():
            keep.wait()

        each(jnp.where(c == 0, 1, c * 4), c * 4 + 4, lambda i: pair(i).wait_recv())
        go(0, c, v).start()
        go(1, c, v).start()
        side(0, c, v).start()

    def b_step(c):
        go(0, c, left).wait_recv()

        @pl.when(c < CHUNKS // 2)
        def _():
            on(0, c, left).start()

        side(2, c, left).start()
        go(1, c, right).wait_recv()

        @pl.when(c >= CHUNKS // 2)
        def _():
            on(1, c, right).start()

        side(1, c, right).start()

    def c_step(c):
        on(0, c, far).wait_recv()
        side(3, c, far).start()

    lag_b, lag_c = 3, 5

    def stage(t):
        @pl.when(t < CHUNKS)
        def _():
            a_step(t)

        @pl.when((t >= lag_b) & (t < CHUNKS + lag_b))
        def _():
            b_step(t - lag_b)

        @pl.when(t >= lag_c)
        def _():
            c_step(t - lag_c)

    each(0, CHUNKS + lag_c, stage)

    across = [mate, right + 1 - 2 * core, left + 1 - 2 * core, far + 1 - 2 * core]
    for kind in range(4):
        each(0, CHUNKS, lambda c: side(kind, c, across[kind]).wait_recv())
    each(1, NV, lambda i: give_best(i, (v + i) % NV).wait_recv())

    each(1, NG, lambda i: tell(i, g).wait_send())
    each(1, NG, lambda i: pair(i).wait_send())
    each(1, NV, lambda i: give_part(i, v).wait_send())
    each(1, NV, lambda i: give_pack(i, v).wait_send())
    each(1, NV, lambda i: give_best(i, v).wait_send())

    @pl.when(v < NV - 1)
    def _():
        give_all(v).wait_send()

    for kind in range(4):
        each(0, CHUNKS, lambda c: side(kind, c, v).wait_send())
    each(0, CHUNKS, lambda c: go(0, c, v).wait_send())
    each(0, CHUNKS, lambda c: go(1, c, v).wait_send())
    each(0, CHUNKS, lambda c: on(0, c, v).wait_send())


def lay_kernel(counts, best, tiles, clones, peak, total, stage, tab, stab, sem):
    g = lax.axis_index("gauss")
    gy, gz = g // 8, g % 8
    sub = lax.broadcasted_iota(jnp.int32, (8, 128), 0)
    k = lax.broadcasted_iota(jnp.int32, (8, 128), 1) * NG + g
    off = jnp.zeros((8, 128), jnp.int32)
    every = jnp.zeros((8, 128), jnp.int32)
    source = jnp.zeros((8, 128), jnp.int32)
    for s in range(NG):
        n = counts[s]
        blocks = (n + (BLK - 1)) >> 7
        where = (((gy - s // 8) & 3) * 8 + ((gz - s % 8) & 7)) * PER
        inside = (k >= off) & (k < off + blocks)
        source = jnp.where(inside, where + ((k - off) >> 5), source)
        off = off + blocks
        every = every + n
    slots = (off - g + (NG - 1)) >> 5
    tab[...] = jnp.where(sub == 0, source, jnp.where(sub == 1, every, slots))
    to_smem = pltpu.make_async_copy(tab, stab, sem.at[0])
    to_smem.start()
    to_smem.wait()
    used = stab[2, 0]
    total[0, 0] = stab[1, 0]

    def cols(at):
        return pl.ds(pl.multiple_of(at * BLK, BLK), BLK)

    def fetch(q):
        return pltpu.make_async_copy(tiles.at[:, cols(stab[0, q])], stage.at[:, cols(q)], sem.at[1])

    each(0, used, lambda q: fetch(q).start())

    def clear(q):
        stage[:, cols(q)] = jnp.zeros((8 * NV, BLK), jnp.float32)

    each(used, CAP, clear)

    def roots(c, _):
        s = pl.ds(pl.multiple_of(c * 1024, 1024), 1024)
        piece, at = c // 2, pl.multiple_of((c % 2) * 8, 8)
        peak[0:1, s] = jnp.sqrt(best[piece, 0, pl.ds(at, 8), :]).reshape(1, 1024)
        peak[1:2, s] = (3.0 * jnp.sqrt(best[piece, 1, pl.ds(at, 8), :])).reshape(1, 1024)
        return 0

    lax.fori_loop(0, 16, roots, 0)
    each(0, used, lambda q: fetch(q).wait())

    puts = []
    for r in range(NV):
        lo, hi = 8 * r, min(8 * r + 8, ROWS)
        puts.append(pltpu.make_async_copy(stage.at[lo:hi, :], clones.at[lo:hi, :], sem.at[2 + r]))
    for put in puts:
        put.start()
    for put in puts:
        put.wait()


def body(means, scales, quats, attrs, grad_screen, visible, clone_mask, rotation, shift, focal):
    f32, i32 = jnp.float32, jnp.int32
    shape = jax.ShapeDtypeStruct
    dma = pltpu.SemaphoreType.DMA
    mask = clone_mask.reshape(128, 128)
    part, packed, tiles, count = pl.pallas_call(
        front_kernel,
        in_specs=[VMEM] * 6 + [SMEM] * 3 + [ANY],
        out_specs=(VMEM,) * 4,
        out_shape=(
            shape((NV, 2, 16, 128), f32),
            shape((CAP, 2, 128), f32),
            shape((CAP, 8, 128), f32),
            shape((8, 128), i32),
        ),
        scratch_shapes=[
            pltpu.VMEM((8, G), f32),
            pltpu.VMEM((8, G), f32),
            pltpu.VMEM((8, G), f32),
            pltpu.VMEM((8, G), f32),
            pltpu.VMEM((128, 128), i32),
            pltpu.VMEM((8, 128), i32),
            pltpu.SMEM((8, 128), i32),
            dma((3,)),
        ],
        compiler_params=pltpu.CompilerParams(vmem_limit_bytes=16 * 2**20),
        name="front",
    )(mask, means, scales, quats, grad_screen, visible, rotation.transpose(1, 0, 2), shift, focal, attrs)

    out, best, counts = pl.pallas_call(
        move_kernel,
        in_specs=[VMEM] * 4,
        out_specs=(ANY, VMEM, VMEM),
        out_shape=(
            shape((8 * NV, G), f32),
            shape((NV, 2, 16, 128), f32),
            shape((NG, 8, 128), i32),
        ),
        scratch_shapes=[
            pltpu.VMEM((NV, 2, 16, 128), f32),
            pltpu.VMEM((NV, 16, 2, 128), f32),
            pltpu.VMEM((2, 16, 128), f32),
            pltpu.VMEM((16, 2, 128), f32),
            pltpu.VMEM((CAP, 2, 128), f32),
            pltpu.VMEM((8, G), f32),
            pltpu.VMEM((8, 128), i32),
            pltpu.SMEM((8, 128), i32),
        ]
        + [dma((NV,))] * 6
        + [dma((1,)), dma((NV,))]
        + [dma((NG,))] * 4
        + [dma((2, CHUNKS)), dma((2, CHUNKS)), dma((4, CHUNKS)), dma((4, CHUNKS)), dma((CHUNKS,)), dma((CHUNKS,))]
        + [dma((2,))],
        compiler_params=pltpu.CompilerParams(
            collective_id=0, has_side_effects=True, vmem_limit_bytes=16 * 2**20
        ),
        name="move",
    )(part, packed, tiles, count)

    clones, peak, total = pl.pallas_call(
        lay_kernel,
        in_specs=[VMEM, VMEM, ANY],
        out_specs=(ANY, VMEM, SMEM),
        out_shape=(shape((ROWS, G), f32), shape((2, G), f32), shape((1, 1), i32)),
        scratch_shapes=[
            pltpu.VMEM((8 * NV, G), f32),
            pltpu.VMEM((8, 128), i32),
            pltpu.SMEM((8, 128), i32),
            dma((2 + NV,)),
        ],
        compiler_params=pltpu.CompilerParams(vmem_limit_bytes=16 * 2**20),
        name="lay",
    )(counts, best, out)
    return (peak, clones, total.reshape(()))


def solution(mesh):
    return jax.shard_map(
        body,
        mesh=mesh,
        in_specs=(
            P(None, "gauss"),
            P(None, "gauss"),
            P(None, "gauss"),
            P(None, "gauss"),
            P("view", None, "gauss"),
            P("view", "gauss"),
            P("gauss"),
            P("view", None, None),
            P("view", None),
            P("view"),
        ),
        out_specs=(P(None, "gauss"), P(None, "gauss"), P()),
        check_vma=False,
    )
```

time: 329 us -> 74.5 us (0.23)
  local copies, waits for them, and re-layouts: 113 us -> 9.74 us
  other arithmetic: 87.1 us -> 0 us
  Pallas kernels: 0 us -> 63.8 us
  waiting for transfers between devices: 52.4 us -> 0 us
  starting transfers between devices: 36.1 us -> 0 us
  between operations: 21.3 us -> 0.67 us
  blocking collectives: 16.9 us -> 0 us
    add x16 -> x0, other arithmetic: 68.8 us -> none  [the longest x8 58.6 us: view_stats(): first = [j00 * rot[0, j] + j02 * rot[2, j] for j in range(3)]]
    pallas_call x0 -> x3, Pallas kernels: none -> 63.8 us  [the longest x1 53.4 us: body(): pl.pallas_call(move_kernel, in_specs=[VMEM] * 4, out_specs=(ANY, VMEM, VM...]
    scatter x2 -> x0, local copies, waits for them, and re-layouts: 48.9 us -> none  [the longest x1 44.3 us: body(): jnp.zeros((feat_rows, cap_blk * 128), jnp.float32).at[:, where_to]]
    all_to_all x4 -> x0, starting transfers between devices: 36 us -> none  [the longest x2 17.3 us: copy_for_each(): lax.all_to_all(jnp.broadcast_to(x[None], (count, *x.shape)), axis, 0, 0,...]
    all_gather x1 -> x0, waiting for transfers between devices: 32.5 us -> none  [body(): placed = lax.all_gather(partial_place, 'view', axis=2, tiled=True)]
    concatenate x2 -> x0, local copies, waits for them, and re-layouts: 28.5 us -> none  [body(): rows = jnp.concatenate([means, scales, quats, attrs, peak], axis=0)]
    all_to_all x4 -> x0, waiting for transfers between devices: 19.8 us -> none  [the longest x1 11.3 us: body(): lax.all_to_all(portion, 'gauss', split_axis=1, concat_axis=1, tiled=True)]
    all_to_all x1 -> x0, blocking collectives: 16.9 us -> none  [copy_for_each(): lax.all_to_all(jnp.broadcast_to(x[None], (count, *x.shape)), axis, 0, 0,...]
  transfers between devices with their start and end apart: 5 -> 0, of which waited for: 3 -> 0; matrix products, arithmetic and copies ran while one was open for 54% -> 0% of each run, Pallas kernels for 0% -> 0%
where the time goes in v2:
time: 74.5 us; the launch traced here: 74.2 us
  Pallas kernels  63.8 us (86%)
  local copies, waits for them, and re-layouts  9.74 us (13%)
    pallas_call x1, Pallas kernels, body(): pl.pallas_call(move_kernel, in_specs=[VMEM] * 4, out_specs=(ANY, VMEM, VM...  53.4 us
    unnamed x20, local copies, waits for them, and re-layouts  9.74 us
    pallas_call x1, Pallas kernels, body(): pl.pallas_call(front_kernel, in_specs=[VMEM] * 6 + [SMEM] * 3 + [ANY], ou...  5.27 us
    pallas_call x1, Pallas kernels, body(): pl.pallas_call(lay_kernel, in_specs=[VMEM, VMEM, ANY], out_specs=(ANY, VM...  5.08 us

profile of v2, /device:TPU:1, one launch (start us, length us, event | category | flops | bytes accessed | tf_op | source)
XLA Modules:
  0.0 74.2 jit_solution(7295799735427068163)
XLA Ops:
  0.6 0.0 copy-start
  0.6 2.0 %copy-done = f32[49,16384]{1,0:T(8,128)S(1)} copy-done((f32[49,16384]{1,0:T(8,128)S(1)}, f32[49,16384]{1,0:T(8,128)}, u32[]{:S(2)}) %copy-start) | copy-done | bytes 3211288
  2.7 0.0 copy-start.1
  2.7 1.0 %copy-done.1 = f32[4,2,16384]{2,1,0:T(2,128)S(1)} copy-done((f32[4,2,16384]{2,1,0:T(2,128)S(1)}, f32[4,2,16384]{2,1,0:T(2,128)}, u32[]{:S(2)}) %copy-start.1) | copy-done | bytes 524312
  3.7 0.0 copy-start.2
  3.7 0.9 %copy-done.2 = f32[3,16384]{1,0:T(4,128)S(1)} copy-done((f32[3,16384]{1,0:T(4,128)S(1)}, f32[3,16384]{1,0:T(4,128)}, u32[]{:S(2)}) %copy-start.2) | copy-done | bytes 196632
  4.7 0.0 copy-start.3
  4.7 0.9 %copy-done.3 = f32[3,16384]{1,0:T(4,128)S(1)} copy-done((f32[3,16384]{1,0:T(4,128)S(1)}, f32[3,16384]{1,0:T(4,128)}, u32[]{:S(2)}) %copy-start.3) | copy-done | bytes 196632
  5.6 0.0 copy-start.4
  5.6 0.9 %copy-done.4 = f32[4,16384]{1,0:T(4,128)S(1)} copy-done((f32[4,16384]{1,0:T(4,128)S(1)}, f32[4,16384]{1,0:T(4,128)}, u32[]{:S(2)}) %copy-start.4) | copy-done | bytes 262168
  6.6 0.0 copy-start.5
  6.6 0.9 %copy-done.5 = s32[4,16384]{1,0:T(4,128)S(1)} copy-done((s32[4,16384]{1,0:T(4,128)S(1)}, s32[4,16384]{1,0:T(4,128)}, u32[]{:S(2)}) %copy-start.5) | copy-done | bytes 262168
  7.5 0.0 copy-start.6
  7.5 0.8 %copy-done.6 = s32[16384]{0:T(1024)S(1)} copy-done((s32[16384]{0:T(1024)S(1)}, s32[16384]{0:T(1024)}, u32[]{:S(2)}) %copy-start.6) | copy-done | bytes 65560
  8.4 0.0 copy-start.7
  8.4 0.7 copy-done.7
  9.1 0.0 copy-start.8
  9.1 0.7 copy-done.8
  9.7 0.0 copy-start.9
  9.7 0.7 copy-done.9
  10.4 5.3 %front.1 = (f32[8,2,16,128]{3,2,1,0:T(8,128)S(1)}, f32[128,2,128]{2,1,0:T(2,128)S(1)}, f32[128,8,128]{2,1,0:T(8,128)S(1)}, s32[8,128]{1,0:T(8,128)S(1)}) custom-call(s32[128,128]{1,0:T(8,128)S(1)} %bitcast.3, f32[3,16384]{1,0:T(4,128)S(1)} %copy-done.2, f32[3,16384]{1,0:T(4,128)S(1)} %copy-done.3, f32[4,16384]{1,0:T(4,128)S(1)} %copy-done.4, ...), custom_call_target="tpu_custom_call" | custom-call | tf_op jit(solution)/shard_map/front/pallas_call | solution.py:466
  15.7 53.4 %move.1 = (f32[64,16384]{1,0:T(8,128)S(1)}, f32[8,2,16,128]{3,2,1,0:T(8,128)S(1)}, s32[32,8,128]{2,1,0:T(8,128)S(1)}) custom-call(f32[8,2,16,128]{3,2,1,0:T(8,128)S(1)} %get-tuple-element.13.part, f32[128,2,128]{2,1,0:T(2,128)S(1)} %get-tuple-element.14.packed, f32[128,8,128]{2,1,0:T(8,128)S(1)} %get-tuple-element.15.tiles, s32[8,128]{1,0:T(8,128)S(1)} %get-tuple-element.16.count), custom_call_target="tpu_custom_call" | custom-call | tf_op jit(solution)/shard_map/move/pallas_call | solution.py:490
  69.1 5.1 %lay.1 = (f32[61,16384]{1,0:T(8,128)}, f32[2,16384]{1,0:T(2,128)}, s32[1,1]{1,0:T(1,128)}) custom-call(s32[32,8,128]{2,1,0:T(8,128)S(1)} %get-tuple-element.17.counts, f32[8,2,16,128]{3,2,1,0:T(8,128)S(1)} %get-tuple-element.18.best, f32[64,16384]{1,0:T(8,128)S(1)} %get-tuple-element.19.tiles), custom_call_target="tpu_custom_call" | custom-call | tf_op jit(solution)/shard_map/lay/pallas_call | solution.py:520
Async XLA Ops:
  0.6 2.0 %copy-start = (f32[49,16384]{1,0:T(8,128)S(1)}, f32[49,16384]{1,0:T(8,128)}, u32[]{:S(2)}) copy-start(f32[49,16384]{1,0:T(8,128)} %attrs.1) | copy-start | bytes 9633796
  2.7 1.0 %copy-start.1 = (f32[4,2,16384]{2,1,0:T(2,128)S(1)}, f32[4,2,16384]{2,1,0:T(2,128)}, u32[]{:S(2)}) copy-start(f32[4,2,16384]{2,1,0:T(2,128)} %grad.1) | copy-start | bytes 1572868
  3.7 0.9 %copy-start.2 = (f32[3,16384]{1,0:T(4,128)S(1)}, f32[3,16384]{1,0:T(4,128)}, u32[]{:S(2)}) copy-start(f32[3,16384]{1,0:T(4,128)} %means.1) | copy-start | bytes 589828
  4.7 0.9 %copy-start.3 = (f32[3,16384]{1,0:T(4,128)S(1)}, f32[3,16384]{1,0:T(4,128)}, u32[]{:S(2)}) copy-start(f32[3,16384]{1,0:T(4,128)} %scales.1) | copy-start | bytes 589828
  5.6 0.9 %copy-start.4 = (f32[4,16384]{1,0:T(4,128)S(1)}, f32[4,16384]{1,0:T(4,128)}, u32[]{:S(2)}) copy-start(f32[4,16384]{1,0:T(4,128)} %quats.1) | copy-start | bytes 786436
  6.6 0.9 %copy-start.5 = (s32[4,16384]{1,0:T(4,128)S(1)}, s32[4,16384]{1,0:T(4,128)}, u32[]{:S(2)}) copy-start(s32[4,16384]{1,0:T(4,128)} %seen.1) | copy-start | bytes 786436
  7.5 0.8 %copy-start.6 = (s32[16384]{0:T(1024)S(1)}, s32[16384]{0:T(1024)}, u32[]{:S(2)}) copy-start(s32[16384]{0:T(1024)} %param.16) | copy-start | bytes 196612
  8.4 0.7 copy-start.7
  9.1 0.7 copy-start.8
  9.7 0.7 copy-start.9

commit v3 on v2

--- a/solution.py
+++ b/solution.py
@@ -15,10 +15,12 @@
 PAIR = PER * BLK
 CHUNKS = 8
 WIDE = G // CHUNKS
+LAG_B, LAG_C = 3, 5
 MESH = pl.DeviceIdType.MESH
 VMEM = pl.BlockSpec(memory_space=pltpu.VMEM)
 SMEM = pl.BlockSpec(memory_space=pltpu.SMEM)
 ANY = pl.BlockSpec(memory_space=pl.ANY)
+HBM = pl.BlockSpec(memory_space=pltpu.HBM)
 
 
 def each(lo, n, do):
@@ -30,11 +32,19 @@
 
 
 def front_kernel(
-    mask, means, scales, quats, grad, seen, rot, trans, focal, attrs,
-    part, packed, tiles, count,
-    xa, xb, x, gl, picks, tab, stab, sem,
+    mask_h, means_h, scales_h, quats_h, grad_h, seen_h, rot_h, trans_h, focal_h, attrs,
+    part, packed, tiles, count, blank,
+    mask, means, scales, quats, grad, seen, rot, trans, focal,
+    xa, xb, x, gl, picks, tab, stab, zeros, sem, load_sem, blank_sem,
 ):
     v = lax.axis_index("view")
+    pairs = (
+        (mask_h, mask), (rot_h, rot), (trans_h, trans), (focal_h, focal), (means_h, means), (scales_h, scales),
+        (quats_h, quats), (seen_h, seen), (grad_h, grad),
+    )
+    loads = [pltpu.make_async_copy(src, dst, load_sem.at[i]) for i, (src, dst) in enumerate(pairs)]
+    for load in loads:
+        load.start()
     a_at = pl.multiple_of(jnp.clip(v - 2, 0, 5) * 8, 8)
     b_at = pl.multiple_of(jnp.clip(v - 1, 0, 5) * 8, 8)
     load_a = pltpu.make_async_copy(attrs.at[pl.ds(a_at, 8), :], xa, sem.at[0])
@@ -49,6 +59,13 @@
     @pl.when(v == 7)
     def _():
         load_c.start()
+
+    zeros[...] = jnp.zeros_like(zeros)
+    fills = []
+    for r in range(NV):
+        lo, hi = 8 * r, min(8 * r + 8, ROWS)
+        fills.append(pltpu.make_async_copy(zeros.at[0 : hi - lo, :], blank.at[lo:hi, :], blank_sem.at[r]))
+    loads[0].wait()
 
     sub = lax.broadcasted_iota(jnp.int32, (8, 128), 0)
     lane = lax.broadcasted_iota(jnp.int32, (8, 128), 1)
@@ -83,6 +100,11 @@
     for bit in range(7):
         e = jnp.where((turn & (1 << bit)) != 0, pltpu.roll(e, 1 << bit, axis=1), e)
     picks[...] = e | jnp.where(i1 < turn, 256, 0)
+
+    for load in loads[1:]:
+        load.wait()
+    for fill in fills:
+        fill.start()
 
     def step(c, _):
         s = pl.ds(pl.multiple_of(c * 1024, 1024), 1024)
@@ -191,12 +213,15 @@
         tiles[last >> 7] = left[0]
         packed[last >> 7] = left[1][0:2]
 
+    for fill in fills:
+        fill.wait()
+
 
 def move_kernel(
     part, packed, tiles, count,
-    out, best, counts,
-    taken, takenp, merged, mergedp, allp, turned, tab, stab,
-    s_part, r_part, s_pack, r_pack, s_best, r_best, s_all, r_all, s_count, r_count, s_pair, r_pair,
+    out, peaks, best, counts,
+    taken, takenp, merged, mergedp, ownp, turned, turnedp, tab, stab,
+    s_part, r_part, s_pack, r_pack, s_best, r_best, s_peak, r_peak, s_count, r_count, s_pair, r_pair, s_top, r_top,
     s_own, r_own, s_side, r_side, s_far, r_far, own,
 ):
     v, g = lax.axis_index("view"), lax.axis_index("gauss")
@@ -213,6 +238,12 @@
     def over_gauss(peer, src, dst, s, r):
         return pltpu.make_async_remote_copy(src, dst, s, r, device_id={"gauss": peer}, device_id_type=MESH)
 
+    def span(at, size):
+        return pl.ds(pl.multiple_of(at * size, size), size)
+
+    def owner(i):
+        return ((gy + i // 8) % 4) * 8 + (gz + i % 8) % 8
+
     def tell(i, slot):
         return over_gauss((g + i) % NG, count, counts.at[slot], s_count.at[i], r_count.at[slot])
 
@@ -220,19 +251,21 @@
         peer = (v + i) % NV
         return over_view(peer, part.at[peer], taken.at[slot], s_part.at[i], r_part.at[slot])
 
+    def give_best(i, slot):
+        return over_view((v + i) % NV, merged, best.at[slot], s_best.at[i], r_best.at[slot])
+
     def give_pack(i, slot):
         peer = (v + i) % NV
-        src = packed.at[pl.ds(peer * 16, 16)]
-        return over_view(peer, src, takenp.at[slot], s_pack.at[i], r_pack.at[slot])
-
-    def give_best(i, slot):
-        return over_view((v + i) % NV, merged, best.at[slot], s_best.at[i], r_best.at[slot])
-
-    def give_all(slot):
-        return over_view(NV - 1, mergedp, allp.at[pl.ds(slot * 16, 16)], s_all.at[0], r_all.at[slot])
+        return over_view(peer, turnedp.at[pl.ds(peer * 16, 16)], takenp.at[slot], s_pack.at[i], r_pack.at[slot])
+
+    def give_top(t):
+        at = pl.ds(t * PER, PER)
+        return over_gauss(owner(v * 4 + t), mergedp.at[at], ownp.at[at], s_top.at[t], r_top.at[t])
+
+    def give_peak(i, slot):
+        return over_view((v + i) % NV, ownp, peaks.at[pl.ds(slot * 16, 16)], s_peak.at[i], r_peak.at[slot])
 
     each(1, NG, lambda i: tell(i, g).start())
-    each(1, NV, lambda i: give_pack(i, v).start())
     each(1, NV, lambda i: give_part(i, v).start())
     counts[g] = count[...]
     each(1, NG, lambda i: tell(i, (g + i) % NG).wait_recv())
@@ -248,71 +281,21 @@
 
     rows = pl.ds(pl.multiple_of(v * 8, 8), 8)
 
-    def span(at, size):
-        return pl.ds(pl.multiple_of(at * size, size), size)
-
-    def owner(i):
-        return ((gy + i // 8) % 4) * 8 + (gz + i % 8) % 8
-
     def pair(i):
         return over_gauss(owner(i), turned.at[:, span(i, PAIR)], out.at[rows, span(i, PAIR)], s_pair.at[i], r_pair.at[i])
 
     keep = pltpu.make_async_copy(turned.at[:, 0:PAIR], out.at[rows, 0:PAIR], own.at[1])
 
-    def turn(finish):
-        def one(i, _):
-            block = (owner(i) - shift) & (NG - 1)
-            for w in range(PER):
-                tile = finish(tiles[block + w * NG], block + w * NG)
-                turned[:, span(i * PER + w, BLK)] = tile
-            return 0
-
-        lax.fori_loop(0, NG, one, 0)
-        each(1, NG, lambda i: pair(i).start())
-        keep.start()
-
-    @pl.when(v < NV - 1)
-    def _():
-        turn(lambda tile, block: tile)
-
-    each(1, NV, lambda i: give_pack(i, (v + i) % NV).wait_recv())
-
-    def merge_p(i, top):
-        return jnp.maximum(top, takenp[(v + i) % NV])
-
-    topp = lax.fori_loop(1, NV, merge_p, packed[pl.ds(v * 16, 16)])
-    mergedp[...] = topp
-
-    @pl.when(v < NV - 1)
-    def _():
-        give_all(v).start()
-
-    @pl.when(v == NV - 1)
-    def _():
-        allp[pl.ds(v * 16, 16)] = topp
-
-    each(1, NV, lambda i: give_part(i, (v + i) % NV).wait_recv())
-
-    def merge(i, top):
-        return jnp.maximum(top, taken[(v + i) % NV])
-
-    top = lax.fori_loop(1, NV, merge, part[v])
-    merged[...] = top
-    best[v] = top
-    each(1, NV, lambda i: give_best(i, v).start())
-
-    @pl.when(v == NV - 1)
-    def _():
-        each(0, NV - 1, lambda i: give_all(i).wait_recv())
-        sub = lax.broadcasted_iota(jnp.int32, (8, 128), 0)
-
-        def finish(tile, block):
-            pair_rows = allp[block]
-            gtop = jnp.broadcast_to(jnp.sqrt(pair_rows[0:1]), (8, 128))
-            ltop = jnp.broadcast_to(3.0 * jnp.sqrt(pair_rows[1:2]), (8, 128))
-            return jnp.where(sub == 3, gtop, jnp.where(sub == 4, ltop, tile))
-
-        turn(finish)
+    def turn(i):
+        block = (owner(i) - shift) & (NG - 1)
+        for w in range(PER):
+            turned[:, span(i * PER + w, BLK)] = tiles[block + w * NG]
+            turnedp[i * PER + w] = packed[block + w * NG]
+
+    each(0, NG, turn)
+    each(1, NG, lambda i: pair(i).start())
+    keep.start()
+    each(1, NV, lambda i: give_pack(i, v).start())
 
     mate = chip * 2 + 1 - core
     right, left, far = (((chip + i) % 4) * 2 + core for i in (1, 3, 2))
@@ -333,67 +316,87 @@
         return over_view(peer, *cut(group, c), s_far.at[c], r_far.at[c])
 
     def a_step(c):
-        @pl.when(c == 0)
-        def _():
+        if c == 0:
             keep.wait()
-
-        each(jnp.where(c == 0, 1, c * 4), c * 4 + 4, lambda i: pair(i).wait_recv())
+        each(max(c * 4, 1), c * 4 + 4, lambda i: pair(i).wait_recv())
         go(0, c, v).start()
         go(1, c, v).start()
         side(0, c, v).start()
 
     def b_step(c):
         go(0, c, left).wait_recv()
-
-        @pl.when(c < CHUNKS // 2)
-        def _():
+        if c < CHUNKS // 2:
             on(0, c, left).start()
-
         side(2, c, left).start()
         go(1, c, right).wait_recv()
-
-        @pl.when(c >= CHUNKS // 2)
-        def _():
+        if c >= CHUNKS // 2:
             on(1, c, right).start()
-
         side(1, c, right).start()
 
     def c_step(c):
         on(0, c, far).wait_recv()
         side(3, c, far).start()
 
-    lag_b, lag_c = 3, 5
-
-    def stage(t):
-        @pl.when(t < CHUNKS)
+    def first():
+        each(1, NV, lambda i: give_part(i, (v + i) % NV).wait_recv())
+        top = lax.fori_loop(1, NV, lambda i, top: jnp.maximum(top, taken[(v + i) % NV]), part[v])
+        merged[...] = top
+        best[v] = top
+        each(1, NV, lambda i: give_best(i, v).start())
+
+    def second():
+        each(1, NV, lambda i: give_pack(i, (v + i) % NV).wait_recv())
+        top = lax.fori_loop(1, NV, lambda i, top: jnp.maximum(top, takenp[(v + i) % NV]), turnedp[pl.ds(v * 16, 16)])
+        mergedp[...] = top
+
+        @pl.when(v > 0)
         def _():
+            give_top(0).start()
+
+        @pl.when(v == 0)
+        def _():
+            ownp[0:PER] = top[0:PER]
+
+        each(1, 4, lambda t: give_top(t).start())
+
+    def third():
+        @pl.when(v > 0)
+        def _():
+            give_top(0).wait_recv()
+
+        each(1, 4, lambda t: give_top(t).wait_recv())
+        peaks[pl.ds(v * 16, 16)] = ownp[...]
+        each(1, NV, lambda i: give_peak(i, v).start())
+
+    between = {0: first, 2: second, 5: third}
+    for t in range(CHUNKS + LAG_C):
+        if t < CHUNKS:
             a_step(t)
-
-        @pl.when((t >= lag_b) & (t < CHUNKS + lag_b))
-        def _():
-            b_step(t - lag_b)
-
-        @pl.when(t >= lag_c)
-        def _():
-            c_step(t - lag_c)
-
-    each(0, CHUNKS + lag_c, stage)
+        if LAG_B <= t < CHUNKS + LAG_B:
+            b_step(t - LAG_B)
+        if LAG_C <= t:
+            c_step(t - LAG_C)
+        if t in between:
+            between[t]()
 
     across = [mate, right + 1 - 2 * core, left + 1 - 2 * core, far + 1 - 2 * core]
     for kind in range(4):
         each(0, CHUNKS, lambda c: side(kind, c, across[kind]).wait_recv())
     each(1, NV, lambda i: give_best(i, (v + i) % NV).wait_recv())
+    each(1, NV, lambda i: give_peak(i, (v + i) % NV).wait_recv())
 
     each(1, NG, lambda i: tell(i, g).wait_send())
     each(1, NG, lambda i: pair(i).wait_send())
     each(1, NV, lambda i: give_part(i, v).wait_send())
     each(1, NV, lambda i: give_pack(i, v).wait_send())
     each(1, NV, lambda i: give_best(i, v).wait_send())
-
-    @pl.when(v < NV - 1)
-    def _():
-        give_all(v).wait_send()
-
+    each(1, NV, lambda i: give_peak(i, v).wait_send())
+
+    @pl.when(v > 0)
+    def _():
+        give_top(0).wait_send()
+
+    each(1, 4, lambda t: give_top(t).wait_send())
     for kind in range(4):
         each(0, CHUNKS, lambda c: side(kind, c, v).wait_send())
     each(0, CHUNKS, lambda c: go(0, c, v).wait_send())
@@ -401,7 +404,8 @@
     each(0, CHUNKS, lambda c: on(0, c, v).wait_send())
 
 
-def lay_kernel(counts, best, tiles, clones, peak, total, stage, tab, stab, sem):
+def lay_kernel(counts, best, peaks, tiles, blank, clones, peak, total, stage, tab, stab, sem):
+    del blank
     g = lax.axis_index("gauss")
     gy, gz = g // 8, g % 8
     sub = lax.broadcasted_iota(jnp.int32, (8, 128), 0)
@@ -428,15 +432,24 @@
     def cols(at):
         return pl.ds(pl.multiple_of(at * BLK, BLK), BLK)
 
-    def fetch(q):
-        return pltpu.make_async_copy(tiles.at[:, cols(stab[0, q])], stage.at[:, cols(q)], sem.at[1])
-
-    each(0, used, lambda q: fetch(q).start())
-
-    def clear(q):
-        stage[:, cols(q)] = jnp.zeros((8 * NV, BLK), jnp.float32)
-
-    each(used, CAP, clear)
+    def put(q):
+        return pltpu.make_async_copy(tiles.at[0:56, cols(stab[0, q])], clones.at[0:56, cols(q)], sem.at[1])
+
+    def put_last(q):
+        return pltpu.make_async_copy(stage.at[0 : ROWS - 56, cols(q)], clones.at[56:ROWS, cols(q)], sem.at[2])
+
+    each(0, used, lambda q: put(q).start())
+
+    def finish(q):
+        at = stab[0, q]
+        tops = peaks[at]
+        gtop = jnp.broadcast_to(jnp.sqrt(tops[0:1]), (8, 128))
+        ltop = jnp.broadcast_to(3.0 * jnp.sqrt(tops[1:2]), (8, 128))
+        tile = tiles[56:64, cols(at)]
+        stage[:, cols(q)] = jnp.where(sub == 3, gtop, jnp.where(sub == 4, ltop, tile))
+
+    each(0, used, finish)
+    each(0, used, lambda q: put_last(q).start())
 
     def roots(c, _):
         s = pl.ds(pl.multiple_of(c * 1024, 1024), 1024)
@@ -446,16 +459,8 @@
         return 0
 
     lax.fori_loop(0, 16, roots, 0)
-    each(0, used, lambda q: fetch(q).wait())
-
-    puts = []
-    for r in range(NV):
-        lo, hi = 8 * r, min(8 * r + 8, ROWS)
-        puts.append(pltpu.make_async_copy(stage.at[lo:hi, :], clones.at[lo:hi, :], sem.at[2 + r]))
-    for put in puts:
-        put.start()
-    for put in puts:
-        put.wait()
+    each(0, used, lambda q: put(q).wait())
+    each(0, used, lambda q: put_last(q).wait())
 
 
 def body(means, scales, quats, attrs, grad_screen, visible, clone_mask, rotation, shift, focal):
@@ -463,17 +468,27 @@
     shape = jax.ShapeDtypeStruct
     dma = pltpu.SemaphoreType.DMA
     mask = clone_mask.reshape(128, 128)
-    part, packed, tiles, count = pl.pallas_call(
+    part, packed, tiles, count, blank = pl.pallas_call(
         front_kernel,
-        in_specs=[VMEM] * 6 + [SMEM] * 3 + [ANY],
-        out_specs=(VMEM,) * 4,
+        in_specs=[HBM] * 10,
+        out_specs=(VMEM,) * 4 + (HBM,),
         out_shape=(
             shape((NV, 2, 16, 128), f32),
             shape((CAP, 2, 128), f32),
             shape((CAP, 8, 128), f32),
             shape((8, 128), i32),
+            shape((ROWS, G), f32),
         ),
         scratch_shapes=[
+            pltpu.VMEM((128, 128), i32),
+            pltpu.VMEM((3, G), f32),
+            pltpu.VMEM((3, G), f32),
+            pltpu.VMEM((4, G), f32),
+            pltpu.VMEM((4, 2, G), f32),
+            pltpu.VMEM((4, G), i32),
+            pltpu.SMEM((3, 4, 3), f32),
+            pltpu.SMEM((4, 3), f32),
+            pltpu.SMEM((4,), f32),
             pltpu.VMEM((8, G), f32),
             pltpu.VMEM((8, G), f32),
             pltpu.VMEM((8, G), f32),
@@ -481,18 +496,27 @@
             pltpu.VMEM((128, 128), i32),
             pltpu.VMEM((8, 128), i32),
             pltpu.SMEM((8, 128), i32),
+            pltpu.VMEM((8, G), f32),
             dma((3,)),
+            dma((9,)),
+            dma((NV,)),
         ],
         compiler_params=pltpu.CompilerParams(vmem_limit_bytes=16 * 2**20),
         name="front",
-    )(mask, means, scales, quats, grad_screen, visible, rotation.transpose(1, 0, 2), shift, focal, attrs)
-
-    out, best, counts = pl.pallas_call(
+    )(
+        *(
+            pltpu.with_memory_space_constraint(a, pltpu.HBM)
+            for a in (mask, means, scales, quats, grad_screen, visible, rotation.transpose(1, 0, 2), shift, focal, attrs)
+        )
+    )
+
+    out, peaks, best, counts = pl.pallas_call(
         move_kernel,
         in_specs=[VMEM] * 4,
-        out_specs=(ANY, VMEM, VMEM),
+        out_specs=(VMEM, VMEM, VMEM, VMEM),
         out_shape=(
             shape((8 * NV, G), f32),
+            shape((CAP, 2, 128), f32),
             shape((NV, 2, 16, 128), f32),
             shape((NG, 8, 128), i32),
         ),
@@ -501,14 +525,15 @@
             pltpu.VMEM((NV, 16, 2, 128), f32),
             pltpu.VMEM((2, 16, 128), f32),
             pltpu.VMEM((16, 2, 128), f32),
+            pltpu.VMEM((16, 2, 128), f32),
+            pltpu.VMEM((8, G), f32),
             pltpu.VMEM((CAP, 2, 128), f32),
-            pltpu.VMEM((8, G), f32),
             pltpu.VMEM((8, 128), i32),
             pltpu.SMEM((8, 128), i32),
         ]
-        + [dma((NV,))] * 6
-        + [dma((1,)), dma((NV,))]
+        + [dma((NV,))] * 8
         + [dma((NG,))] * 4
+        + [dma((4,))] * 2
         + [dma((2, CHUNKS)), dma((2, CHUNKS)), dma((4, CHUNKS)), dma((4, CHUNKS)), dma((CHUNKS,)), dma((CHUNKS,))]
         + [dma((2,))],
         compiler_params=pltpu.CompilerParams(
@@ -519,18 +544,19 @@
 
     clones, peak, total = pl.pallas_call(
         lay_kernel,
-        in_specs=[VMEM, VMEM, ANY],
-        out_specs=(ANY, VMEM, SMEM),
+        in_specs=[VMEM, VMEM, VMEM, VMEM, HBM],
+        out_specs=(HBM, VMEM, SMEM),
         out_shape=(shape((ROWS, G), f32), shape((2, G), f32), shape((1, 1), i32)),
+        input_output_aliases={4: 0},
         scratch_shapes=[
-            pltpu.VMEM((8 * NV, G), f32),
+            pltpu.VMEM((8, G), f32),
             pltpu.VMEM((8, 128), i32),
             pltpu.SMEM((8, 128), i32),
-            dma((2 + NV,)),
+            dma((3,)),
         ],
         compiler_params=pltpu.CompilerParams(vmem_limit_bytes=16 * 2**20),
         name="lay",
-    )(counts, best, out)
+    )(counts, best, peaks, out, blank)
     return (peak, clones, total.reshape(()))
 
 

time: 74.5 us -> 63.5 us (0.85)
  local copies, waits for them, and re-layouts: 9.74 us -> 0 us
  Pallas kernels: 63.8 us -> 62.7 us
    unnamed x20 -> x0, local copies, waits for them, and re-layouts: 9.74 us -> none
    pallas_call x3, Pallas kernels: 63.8 us -> 62.7 us  [the longest x1 53.5 us: body(): pl.pallas_call(move_kernel, in_specs=[VMEM] * 4, out_specs=(VMEM, VMEM, V...]
where the time goes in v3:
time: 63.5 us; the launch traced here: 63.3 us
  Pallas kernels  62.7 us (99%)
  between operations  0.65 us (1%)
    pallas_call x1, Pallas kernels, body(): pl.pallas_call(move_kernel, in_specs=[VMEM] * 4, out_specs=(VMEM, VMEM, V...  53.5 us
    pallas_call x1, Pallas kernels, body(): pl.pallas_call(front_kernel, in_specs=[HBM] * 10, out_specs=(VMEM,) * 4 +...  5.55 us
    pallas_call x1, Pallas kernels, body(): pl.pallas_call(lay_kernel, in_specs=[VMEM, VMEM, VMEM, VMEM, HBM], out_sp...  3.57 us

profile of v3, /device:TPU:1, one launch (start us, length us, event | category | flops | bytes accessed | tf_op | source)
XLA Modules:
  0.0 63.3 jit_solution(6258596795241486535)
XLA Ops:
  0.6 5.5 %front.1 = (f32[8,2,16,128]{3,2,1,0:T(8,128)S(1)}, f32[128,2,128]{2,1,0:T(2,128)S(1)}, f32[128,8,128]{2,1,0:T(8,128)S(1)}, s32[8,128]{1,0:T(8,128)S(1)}, f32[61,16384]{1,0:T(8,128)}) custom-call(s32[128,128]{1,0:T(8,128)} %bitcast.3, f32[3,16384]{1,0:T(4,128)} %means_h.1, f32[3,16384]{1,0:T(4,128)} %scales_h.1, f32[4,16384]{1,0:T(4,128)} %quats_h.1, ...), custom_call_target="tpu_custom_call" | custom-call | tf_op jit(solution)/shard_map/front/pallas_call | solution.py:471
  6.2 53.5 %move.1 = (f32[64,16384]{1,0:T(8,128)S(1)}, f32[128,2,128]{2,1,0:T(2,128)S(1)}, f32[8,2,16,128]{3,2,1,0:T(8,128)S(1)}, s32[32,8,128]{2,1,0:T(8,128)S(1)}) custom-call(f32[8,2,16,128]{3,2,1,0:T(8,128)S(1)} %get-tuple-element.15.part, f32[128,2,128]{2,1,0:T(2,128)S(1)} %get-tuple-element.16.packed, f32[128,8,128]{2,1,0:T(8,128)S(1)} %get-tuple-element.17.tiles, ...), custom_call_target="tpu_custom_call" | custom-call | tf_op jit(solution)/shard_map/move/pallas_call | solution.py:513
  59.7 3.6 %lay.1 = (f32[61,16384]{1,0:T(8,128)}, f32[2,16384]{1,0:T(2,128)}, s32[1,1]{1,0:T(1,128)}) custom-call(s32[32,8,128]{2,1,0:T(8,128)S(1)} %get-tuple-element.19.counts, f32[8,2,16,128]{3,2,1,0:T(8,128)S(1)} %get-tuple-element.20.best, f32[128,2,128]{2,1,0:T(2,128)S(1)} %get-tuple-element.21.peaks, ...), custom_call_target="tpu_custom_call", output_to_operand_aliasing={{0}: (4, {})} | custom-call | tf_op jit(solution)/shard_map/lay/pallas_call | solution.py:545

commit v4 on v3

--- a/solution.py
+++ b/solution.py
@@ -1,3 +1,5 @@
+import functools
+
 import jax
 import jax.numpy as jnp
 from jax import lax
@@ -12,18 +14,20 @@
 NV = 8
 NG = 32
 PER = CAP // NG
-PAIR = PER * BLK
-CHUNKS = 8
-WIDE = G // CHUNKS
-LAG_B, LAG_C = 3, 5
+CHUNKS = 4
+SIZES = (32, 40, 48, 56, 64, 96, 128)
 MESH = pl.DeviceIdType.MESH
 VMEM = pl.BlockSpec(memory_space=pltpu.VMEM)
 SMEM = pl.BlockSpec(memory_space=pltpu.SMEM)
-ANY = pl.BlockSpec(memory_space=pl.ANY)
 HBM = pl.BlockSpec(memory_space=pltpu.HBM)
 
 
 def each(lo, n, do):
+    if isinstance(lo, int) and isinstance(n, int):
+        for i in range(lo, n):
+            do(i)
+        return
+
     def one(i, _):
         do(i)
         return 0
@@ -219,13 +223,12 @@
 
 def move_kernel(
     part, packed, tiles, count,
-    out, peaks, best, counts,
-    taken, takenp, merged, mergedp, ownp, turned, turnedp, tab, stab,
-    s_part, r_part, s_pack, r_pack, s_best, r_best, s_peak, r_peak, s_count, r_count, s_pair, r_pair, s_top, r_top,
-    s_own, r_own, s_side, r_side, s_far, r_far, own,
+    mine, top, best, counts, table, kind,
+    taken, takenp, merged, mergedp, turned, turnedp, tab, stab,
+    s_part, r_part, s_pack, r_pack, s_best, r_best, s_count, r_count, s_pair, r_pair, s_top, r_top,
+    own,
 ):
     v, g = lax.axis_index("view"), lax.axis_index("gauss")
-    core, chip = v % 2, v // 2
     gy, gz = g // 8, g % 8
     barrier = pltpu.get_barrier_semaphore()
     each(1, NV, lambda i: pl.semaphore_signal(barrier, inc=1, device_id={"view": (v + i) % NV}, device_id_type=MESH))
@@ -238,9 +241,6 @@
     def over_gauss(peer, src, dst, s, r):
         return pltpu.make_async_remote_copy(src, dst, s, r, device_id={"gauss": peer}, device_id_type=MESH)
 
-    def span(at, size):
-        return pl.ds(pl.multiple_of(at * size, size), size)
-
     def owner(i):
         return ((gy + i // 8) % 4) * 8 + (gz + i % 8) % 8
 
@@ -260,10 +260,7 @@
 
     def give_top(t):
         at = pl.ds(t * PER, PER)
-        return over_gauss(owner(v * 4 + t), mergedp.at[at], ownp.at[at], s_top.at[t], r_top.at[t])
-
-    def give_peak(i, slot):
-        return over_view((v + i) % NV, ownp, peaks.at[pl.ds(slot * 16, 16)], s_peak.at[i], r_peak.at[slot])
+        return over_gauss(owner(v * 4 + t), mergedp.at[at], top.at[at], s_top.at[t], r_top.at[t])
 
     each(1, NG, lambda i: tell(i, g).start())
     each(1, NV, lambda i: give_part(i, v).start())
@@ -279,17 +276,16 @@
     to_smem.wait()
     shift = stab[0, 0]
 
-    rows = pl.ds(pl.multiple_of(v * 8, 8), 8)
-
     def pair(i):
-        return over_gauss(owner(i), turned.at[:, span(i, PAIR)], out.at[rows, span(i, PAIR)], s_pair.at[i], r_pair.at[i])
-
-    keep = pltpu.make_async_copy(turned.at[:, 0:PAIR], out.at[rows, 0:PAIR], own.at[1])
+        at = pl.ds(i * PER, PER)
+        return over_gauss(owner(i), turned.at[at], mine.at[at], s_pair.at[i], r_pair.at[i])
+
+    keep = pltpu.make_async_copy(turned.at[0:PER], mine.at[0:PER], own.at[1])
 
     def turn(i):
         block = (owner(i) - shift) & (NG - 1)
         for w in range(PER):
-            turned[:, span(i * PER + w, BLK)] = tiles[block + w * NG]
+            turned[i * PER + w] = tiles[block + w * NG]
             turnedp[i * PER + w] = packed[block + w * NG]
 
     each(0, NG, turn)
@@ -297,57 +293,17 @@
     keep.start()
     each(1, NV, lambda i: give_pack(i, v).start())
 
-    mate = chip * 2 + 1 - core
-    right, left, far = (((chip + i) % 4) * 2 + core for i in (1, 3, 2))
-
-    def cut(group, c):
-        at = out.at[pl.ds(pl.multiple_of(group * 8, 8), 8), span(c, WIDE)]
-        return at, at
-
-    def side(kind, c, group):
-        return over_view(mate, *cut(group, c), s_side.at[kind, c], r_side.at[kind, c])
-
-    def go(way, c, group):
-        peer = right if way == 0 else left
-        return over_view(peer, *cut(group, c), s_own.at[way, c], r_own.at[way, c])
-
-    def on(way, c, group):
-        peer = right if way == 0 else left
-        return over_view(peer, *cut(group, c), s_far.at[c], r_far.at[c])
-
-    def a_step(c):
-        if c == 0:
-            keep.wait()
-        each(max(c * 4, 1), c * 4 + 4, lambda i: pair(i).wait_recv())
-        go(0, c, v).start()
-        go(1, c, v).start()
-        side(0, c, v).start()
-
-    def b_step(c):
-        go(0, c, left).wait_recv()
-        if c < CHUNKS // 2:
-            on(0, c, left).start()
-        side(2, c, left).start()
-        go(1, c, right).wait_recv()
-        if c >= CHUNKS // 2:
-            on(1, c, right).start()
-        side(1, c, right).start()
-
-    def c_step(c):
-        on(0, c, far).wait_recv()
-        side(3, c, far).start()
-
     def first():
         each(1, NV, lambda i: give_part(i, (v + i) % NV).wait_recv())
-        top = lax.fori_loop(1, NV, lambda i, top: jnp.maximum(top, taken[(v + i) % NV]), part[v])
-        merged[...] = top
-        best[v] = top
+        so_far = lax.fori_loop(1, NV, lambda i, so: jnp.maximum(so, taken[(v + i) % NV]), part[v])
+        merged[...] = so_far
+        best[v] = so_far
         each(1, NV, lambda i: give_best(i, v).start())
 
     def second():
         each(1, NV, lambda i: give_pack(i, (v + i) % NV).wait_recv())
-        top = lax.fori_loop(1, NV, lambda i, top: jnp.maximum(top, takenp[(v + i) % NV]), turnedp[pl.ds(v * 16, 16)])
-        mergedp[...] = top
+        best_p = lax.fori_loop(1, NV, lambda i, so: jnp.maximum(so, takenp[(v + i) % NV]), turnedp[pl.ds(v * 16, 16)])
+        mergedp[...] = best_p
 
         @pl.when(v > 0)
         def _():
@@ -355,7 +311,7 @@
 
         @pl.when(v == 0)
         def _():
-            ownp[0:PER] = top[0:PER]
+            top[0:PER] = best_p[0:PER]
 
         each(1, 4, lambda t: give_top(t).start())
 
@@ -365,49 +321,9 @@
             give_top(0).wait_recv()
 
         each(1, 4, lambda t: give_top(t).wait_recv())
-        peaks[pl.ds(v * 16, 16)] = ownp[...]
-        each(1, NV, lambda i: give_peak(i, v).start())
-
-    between = {0: first, 2: second, 5: third}
-    for t in range(CHUNKS + LAG_C):
-        if t < CHUNKS:
-            a_step(t)
-        if LAG_B <= t < CHUNKS + LAG_B:
-            b_step(t - LAG_B)
-        if LAG_C <= t:
-            c_step(t - LAG_C)
-        if t in between:
-            between[t]()
-
-    across = [mate, right + 1 - 2 * core, left + 1 - 2 * core, far + 1 - 2 * core]
-    for kind in range(4):
-        each(0, CHUNKS, lambda c: side(kind, c, across[kind]).wait_recv())
-    each(1, NV, lambda i: give_best(i, (v + i) % NV).wait_recv())
-    each(1, NV, lambda i: give_peak(i, (v + i) % NV).wait_recv())
-
-    each(1, NG, lambda i: tell(i, g).wait_send())
-    each(1, NG, lambda i: pair(i).wait_send())
-    each(1, NV, lambda i: give_part(i, v).wait_send())
-    each(1, NV, lambda i: give_pack(i, v).wait_send())
-    each(1, NV, lambda i: give_best(i, v).wait_send())
-    each(1, NV, lambda i: give_peak(i, v).wait_send())
-
-    @pl.when(v > 0)
-    def _():
-        give_top(0).wait_send()
-
-    each(1, 4, lambda t: give_top(t).wait_send())
-    for kind in range(4):
-        each(0, CHUNKS, lambda c: side(kind, c, v).wait_send())
-    each(0, CHUNKS, lambda c: go(0, c, v).wait_send())
-    each(0, CHUNKS, lambda c: go(1, c, v).wait_send())
-    each(0, CHUNKS, lambda c: on(0, c, v).wait_send())
-
-
-def lay_kernel(counts, best, peaks, tiles, blank, clones, peak, total, stage, tab, stab, sem):
-    del blank
-    g = lax.axis_index("gauss")
-    gy, gz = g // 8, g % 8
+
+    first()
+
     sub = lax.broadcasted_iota(jnp.int32, (8, 128), 0)
     k = lax.broadcasted_iota(jnp.int32, (8, 128), 1) * NG + g
     off = jnp.zeros((8, 128), jnp.int32)
@@ -422,34 +338,138 @@
         off = off + blocks
         every = every + n
     slots = (off - g + (NG - 1)) >> 5
-    tab[...] = jnp.where(sub == 0, source, jnp.where(sub == 1, every, slots))
-    to_smem = pltpu.make_async_copy(tab, stab, sem.at[0])
-    to_smem.start()
-    to_smem.wait()
-    used = stab[2, 0]
-    total[0, 0] = stab[1, 0]
+    most = (off + (NG - 1)) >> 5
+    pick = sum((most > size).astype(jnp.int32) for size in SIZES[:-1])
+    table[...] = jnp.where(sub == 0, source, jnp.where(sub == 1, every, slots))
+    tab[...] = pick
+    pick_smem = pltpu.make_async_copy(tab, stab, own.at[0])
+    pick_smem.start()
+
+    second()
+    third()
+    pick_smem.wait()
+    kind[0, 0] = stab[0, 0]
+    keep.wait()
+    each(1, NG, lambda i: pair(i).wait_recv())
+    each(1, NV, lambda i: give_best(i, (v + i) % NV).wait_recv())
+
+    each(1, NG, lambda i: tell(i, g).wait_send())
+    each(1, NG, lambda i: pair(i).wait_send())
+    each(1, NV, lambda i: give_part(i, v).wait_send())
+    each(1, NV, lambda i: give_pack(i, v).wait_send())
+    each(1, NV, lambda i: give_best(i, v).wait_send())
+
+    @pl.when(v > 0)
+    def _():
+        give_top(0).wait_send()
+
+    each(1, 4, lambda t: give_top(t).wait_send())
+
+
+def share_kernel(size, mine, table, top, out, peaks, s_own, r_own, s_side, r_side, s_far, r_far, s_peak, r_peak, own):
+    v = lax.axis_index("view")
+    core, chip = v % 2, v // 2
+    mate = chip * 2 + 1 - core
+    right, left, far = (((chip + i) % 4) * 2 + core for i in (1, 3, 2))
+    barrier = pltpu.get_barrier_semaphore()
+    each(1, NV, lambda i: pl.semaphore_signal(barrier, inc=1, device_id={"view": (v + i) % NV}, device_id_type=MESH))
+    rows = pl.ds(pl.multiple_of(v * 8, 8), 8)
 
     def cols(at):
         return pl.ds(pl.multiple_of(at * BLK, BLK), BLK)
 
-    def put(q):
-        return pltpu.make_async_copy(tiles.at[0:56, cols(stab[0, q])], clones.at[0:56, cols(q)], sem.at[1])
-
-    def put_last(q):
-        return pltpu.make_async_copy(stage.at[0 : ROWS - 56, cols(q)], clones.at[56:ROWS, cols(q)], sem.at[2])
-
-    each(0, used, lambda q: put(q).start())
+    def place(q):
+        out[rows, cols(q)] = mine[table[0, q]]
+
+    each(0, size, place)
+    keep = pltpu.make_async_copy(top, peaks.at[pl.ds(v * 16, 16)], own.at[0])
+    keep.start()
+    pl.semaphore_wait(barrier, NV - 1)
+    wide = size * BLK // CHUNKS
+
+    def over_view(peer, group, c, s, r):
+        at = out.at[pl.ds(pl.multiple_of(group * 8, 8), 8), c * wide : (c + 1) * wide]
+        return pltpu.make_async_remote_copy(at, at, s, r, device_id={"view": peer}, device_id_type=MESH)
+
+    def side(kind, c, group):
+        return over_view(mate, group, c, s_side.at[kind, c], r_side.at[kind, c])
+
+    def go(way, c, group):
+        return over_view(right if way == 0 else left, group, c, s_own.at[way, c], r_own.at[way, c])
+
+    def on(way, c, group):
+        return over_view(right if way == 0 else left, group, c, s_far.at[c], r_far.at[c])
+
+    for c in range(CHUNKS):
+        go(0, c, v).start()
+        go(1, c, v).start()
+        side(0, c, v).start()
+    def give_peak(i, slot):
+        return pltpu.make_async_remote_copy(
+            top,
+            peaks.at[pl.ds(slot * 16, 16)],
+            s_peak.at[i],
+            r_peak.at[slot],
+            device_id={"view": (v + i) % NV},
+            device_id_type=MESH,
+        )
+
+    each(1, NV, lambda i: give_peak(i, v).start())
+    for c in range(CHUNKS):
+        go(0, c, left).wait_recv()
+        if c < CHUNKS // 2:
+            on(0, c, left).start()
+        side(2, c, left).start()
+        go(1, c, right).wait_recv()
+        if c >= CHUNKS // 2:
+            on(1, c, right).start()
+        side(1, c, right).start()
+    for c in range(CHUNKS):
+        on(0, c, far).wait_recv()
+        side(3, c, far).start()
+    across = [mate, right + 1 - 2 * core, left + 1 - 2 * core, far + 1 - 2 * core]
+    for c in range(CHUNKS):
+        for kind in range(4):
+            side(kind, c, across[kind]).wait_recv()
+            side(kind, c, v).wait_send()
+        go(0, c, v).wait_send()
+        go(1, c, v).wait_send()
+        on(0, c, v).wait_send()
+    each(1, NV, lambda i: give_peak(i, (v + i) % NV).wait_recv())
+    each(1, NV, lambda i: give_peak(i, v).wait_send())
+    keep.wait()
+
+
+def lay_kernel(size, table, best, peaks, tiles, blank, clones, peak, total, stage, sem):
+    del blank
+    sub = lax.broadcasted_iota(jnp.int32, (8, 128), 0)
+    used = table[2, 0]
+    total[0, 0] = table[1, 0]
+
+    def cols(at):
+        return pl.ds(pl.multiple_of(at * BLK, BLK), BLK)
+
+    def copies(src, dst, sem):
+        for n in (128, 64, 32, 16, 8, 4, 2, 1):
+            at = pl.ds(pl.multiple_of((used & (256 - 2 * n)) * BLK, BLK), n * BLK)
+            if n <= size:
+                yield (used & n) != 0, pltpu.make_async_copy(src.at[:, at], dst.at[:, at], sem)
+
+    main = list(copies(tiles.at[0:56, :], clones.at[0:56, :], sem.at[0]))
+    rest = list(copies(stage.at[0 : ROWS - 56, :], clones.at[56:ROWS, :], sem.at[1]))
+    for on, copy in main:
+        pl.when(on)(copy.start)
 
     def finish(q):
-        at = stab[0, q]
-        tops = peaks[at]
+        tops = peaks[table[0, q]]
         gtop = jnp.broadcast_to(jnp.sqrt(tops[0:1]), (8, 128))
         ltop = jnp.broadcast_to(3.0 * jnp.sqrt(tops[1:2]), (8, 128))
-        tile = tiles[56:64, cols(at)]
+        tile = tiles[56:64, cols(q)]
         stage[:, cols(q)] = jnp.where(sub == 3, gtop, jnp.where(sub == 4, ltop, tile))
 
     each(0, used, finish)
-    each(0, used, lambda q: put_last(q).start())
+    for on, copy in rest:
+        pl.when(on)(copy.start)
 
     def roots(c, _):
         s = pl.ds(pl.multiple_of(c * 1024, 1024), 1024)
@@ -459,8 +479,8 @@
         return 0
 
     lax.fori_loop(0, 16, roots, 0)
-    each(0, used, lambda q: put(q).wait())
-    each(0, used, lambda q: put_last(q).wait())
+    for on, copy in main + rest:
+        pl.when(on)(copy.wait)
 
 
 def body(means, scales, quats, attrs, grad_screen, visible, clone_mask, rotation, shift, focal):
@@ -510,31 +530,31 @@
         )
     )
 
-    out, peaks, best, counts = pl.pallas_call(
+    mine, top, best, _, table, kind = pl.pallas_call(
         move_kernel,
         in_specs=[VMEM] * 4,
-        out_specs=(VMEM, VMEM, VMEM, VMEM),
+        out_specs=(VMEM,) * 5 + (SMEM,),
         out_shape=(
-            shape((8 * NV, G), f32),
-            shape((CAP, 2, 128), f32),
+            shape((CAP, 8, 128), f32),
+            shape((16, 2, 128), f32),
             shape((NV, 2, 16, 128), f32),
             shape((NG, 8, 128), i32),
+            shape((8, 128), i32),
+            shape((1, 1), i32),
         ),
         scratch_shapes=[
             pltpu.VMEM((NV, 2, 16, 128), f32),
             pltpu.VMEM((NV, 16, 2, 128), f32),
             pltpu.VMEM((2, 16, 128), f32),
             pltpu.VMEM((16, 2, 128), f32),
-            pltpu.VMEM((16, 2, 128), f32),
-            pltpu.VMEM((8, G), f32),
+            pltpu.VMEM((CAP, 8, 128), f32),
             pltpu.VMEM((CAP, 2, 128), f32),
             pltpu.VMEM((8, 128), i32),
             pltpu.SMEM((8, 128), i32),
         ]
-        + [dma((NV,))] * 8
+        + [dma((NV,))] * 6
         + [dma((NG,))] * 4
         + [dma((4,))] * 2
-        + [dma((2, CHUNKS)), dma((2, CHUNKS)), dma((4, CHUNKS)), dma((4, CHUNKS)), dma((CHUNKS,)), dma((CHUNKS,))]
         + [dma((2,))],
         compiler_params=pltpu.CompilerParams(
             collective_id=0, has_side_effects=True, vmem_limit_bytes=16 * 2**20
@@ -542,21 +562,41 @@
         name="move",
     )(part, packed, tiles, count)
 
-    clones, peak, total = pl.pallas_call(
-        lay_kernel,
-        in_specs=[VMEM, VMEM, VMEM, VMEM, HBM],
-        out_specs=(HBM, VMEM, SMEM),
-        out_shape=(shape((ROWS, G), f32), shape((2, G), f32), shape((1, 1), i32)),
-        input_output_aliases={4: 0},
-        scratch_shapes=[
-            pltpu.VMEM((8, G), f32),
-            pltpu.VMEM((8, 128), i32),
-            pltpu.SMEM((8, 128), i32),
-            dma((3,)),
-        ],
-        compiler_params=pltpu.CompilerParams(vmem_limit_bytes=16 * 2**20),
-        name="lay",
-    )(counts, best, peaks, out, blank)
+    def share(n, size):
+        gather = pl.pallas_call(
+            functools.partial(share_kernel, size),
+            in_specs=[VMEM, SMEM, VMEM],
+            out_specs=(VMEM, VMEM),
+            out_shape=(shape((8 * NV, size * BLK), f32), shape((CAP, 2, 128), f32)),
+            scratch_shapes=[dma((2, CHUNKS))] * 2
+            + [dma((4, CHUNKS))] * 2
+            + [dma((CHUNKS,))] * 2
+            + [dma((NV,))] * 2
+            + [dma((1,))],
+            compiler_params=pltpu.CompilerParams(
+                collective_id=1 + n, has_side_effects=True, vmem_limit_bytes=16 * 2**20
+            ),
+            name=f"share{size}",
+        )
+        lay = pl.pallas_call(
+            functools.partial(lay_kernel, size),
+            in_specs=[SMEM, VMEM, VMEM, VMEM, HBM],
+            out_specs=(HBM, VMEM, SMEM),
+            out_shape=(shape((ROWS, G), f32), shape((2, G), f32), shape((1, 1), i32)),
+            input_output_aliases={4: 0},
+            scratch_shapes=[pltpu.VMEM((8, size * BLK), f32), dma((2,))],
+            compiler_params=pltpu.CompilerParams(vmem_limit_bytes=16 * 2**20),
+            name=f"lay{size}",
+        )
+        def branch(mine, table, best, top, blank):
+            tiles, peaks = gather(mine, table, top)
+            return lay(table, best, peaks, tiles, pltpu.with_memory_space_constraint(blank, pltpu.HBM))
+
+        return branch
+
+    blank = pltpu.with_memory_space_constraint(blank, pltpu.HBM)
+    branches = [share(n, size) for n, size in enumerate(SIZES)]
+    clones, peak, total = lax.switch(kind.reshape(()), branches, mine, table, best, top, blank)
     return (peak, clones, total.reshape(()))
 
 

time: 63.5 us -> 61.1 us (0.962)
  Pallas kernels: 62.7 us -> 59.6 us
  between operations: 0.65 us -> 1.34 us
    pallas_call x2 -> x3, Pallas kernels: 57.1 us -> 54 us  [the longest x1 34 us: body(): pl.pallas_call(move_kernel, in_specs=[VMEM] * 4, out_specs=(VMEM,) * 5 +...]
where the time goes in v4:
time: 61.1 us; the launch traced here: 61 us
  Pallas kernels  59.6 us (98%)
  between operations  1.34 us (2%)
    pallas_call x1, Pallas kernels, body(): pl.pallas_call(move_kernel, in_specs=[VMEM] * 4, out_specs=(VMEM,) * 5 +...  34 us
    pallas_call x1, Pallas kernels, branch(): tiles, peaks = gather(mine, table, top)  17.5 us
    pallas_call x1, Pallas kernels, body(): pl.pallas_call(front_kernel, in_specs=[HBM] * 10, out_specs=(VMEM,) * 4 +...  5.55 us
    pallas_call x1, Pallas kernels, branch(): lay(table, best, peaks, tiles, pltpu.with_memory_space_constraint(blank,...  2.59 us

profile of v4, /device:TPU:1, one launch (start us, length us, event | category | flops | bytes accessed | tf_op | source)
XLA Modules:
  0.0 61.0 jit_solution(15990393595582000908)
XLA Ops:
  0.6 5.5 %front.1 = (f32[8,2,16,128]{3,2,1,0:T(8,128)S(1)}, f32[128,2,128]{2,1,0:T(2,128)S(1)}, f32[128,8,128]{2,1,0:T(8,128)S(1)}, s32[8,128]{1,0:T(8,128)S(1)}, f32[61,16384]{1,0:T(8,128)}) custom-call(s32[128,128]{1,0:T(8,128)} %bitcast.10, f32[3,16384]{1,0:T(4,128)} %means_h.1, f32[3,16384]{1,0:T(4,128)} %scales_h.1, f32[4,16384]{1,0:T(4,128)} %quats_h.1, ...), custom_call_target="tpu_custom_call" | custom-call | tf_op jit(solution)/shard_map/front/pallas_call | solution.py:491
  6.2 34.0 %move.1 = (f32[128,8,128]{2,1,0:T(8,128)S(1)}, f32[16,2,128]{2,1,0:T(2,128)S(1)}, f32[8,2,16,128]{3,2,1,0:T(8,128)S(1)}, s32[32,8,128]{2,1,0:T(8,128)}, s32[8,128]{1,0:T(8,128)S(1)}, /*index=5*/s32[1,1]{1,0:T(1,128)}) custom-call(f32[8,2,16,128]{3,2,1,0:T(8,128)S(1)} %get-tuple-element.178.part, f32[128,2,128]{2,1,0:T(2,128)S(1)} %get-tuple-element.179.packed, ...), custom_call_target="tpu_custom_call" | custom-call | tf_op jit(solution)/shard_map/move/pallas_call | solution.py:533
  40.9 20.1 %conditional.1 = (f32[61,16384]{1,0:T(8,128)}, f32[2,16384]{1,0:T(2,128)}, s32[]{:T(128)}) conditional(s32[]{:T(128)} %bitcast.9, (f32[128,8,128]{2,1,0:T(8,128)S(1)}, s32[8,128]{1,0:T(8,128)S(1)}, f32[16,2,128]{2,1,0:T(2,128)S(1)}, f32[8,2,16,128]{3,2,1,0:T(8,128)S(1)}, f32[61,16384]{1,0:T(8,128)}) %tuple.43, ...), branch_computations={%region_0.0_spmd, %region_1.0_spmd, %region_2.0_spmd, %region_3.0_... | conditional | bytes 24 | solution.py:599
  40.9 17.5 %share48.1 = (f32[64,6144]{1,0:T(8,128)S(1)}, f32[128,2,128]{2,1,0:T(2,128)S(1)}) custom-call(f32[128,8,128]{2,1,0:T(8,128)S(1)} %get-tuple-element.114.mine, s32[8,128]{1,0:T(8,128)S(1)} %get-tuple-element.112.table, f32[16,2,128]{2,1,0:T(2,128)S(1)} %get-tuple-element.115.top), custom_call_target="tpu_custom_call" | custom-call | tf_op jit(solution)/shard_map/cond/branch_2_fun/share48/pallas_call | solution.py:592
  58.4 2.6 %lay48.1 = (f32[61,16384]{1,0:T(8,128)}, f32[2,16384]{1,0:T(2,128)}, s32[1,1]{1,0:T(1,128)}) custom-call(s32[8,128]{1,0:T(8,128)S(1)} %get-tuple-element.112.table, f32[8,2,16,128]{3,2,1,0:T(8,128)S(1)} %get-tuple-element.113.best, f32[128,2,128]{2,1,0:T(2,128)S(1)} %get-tuple-element.116.peaks, ...), custom_call_target="tpu_custom_call", output_to_operand_aliasing={{0}: (4, {})} | custom-call | tf_op jit(solution)/shard_map/cond/branch_2_fun/lay48/pallas_call | solution.py:593

commit v5 on v4

--- a/solution.py
+++ b/solution.py
@@ -15,7 +15,7 @@
 NG = 32
 PER = CAP // NG
 CHUNKS = 4
-SIZES = (32, 40, 48, 56, 64, 96, 128)
+FIRST = 60
 MESH = pl.DeviceIdType.MESH
 VMEM = pl.BlockSpec(memory_space=pltpu.VMEM)
 SMEM = pl.BlockSpec(memory_space=pltpu.SMEM)
@@ -221,170 +221,19 @@
         fill.wait()
 
 
-def move_kernel(
-    part, packed, tiles, count,
-    mine, top, best, counts, table, kind,
-    taken, takenp, merged, mergedp, turned, turnedp, tab, stab,
-    s_part, r_part, s_pack, r_pack, s_best, r_best, s_count, r_count, s_pair, r_pair, s_top, r_top,
-    own,
-):
-    v, g = lax.axis_index("view"), lax.axis_index("gauss")
-    gy, gz = g // 8, g % 8
-    barrier = pltpu.get_barrier_semaphore()
-    each(1, NV, lambda i: pl.semaphore_signal(barrier, inc=1, device_id={"view": (v + i) % NV}, device_id_type=MESH))
-    each(1, NG, lambda i: pl.semaphore_signal(barrier, inc=1, device_id={"gauss": (g + i) % NG}, device_id_type=MESH))
-    pl.semaphore_wait(barrier, NV - 1 + NG - 1)
-
-    def over_view(peer, src, dst, s, r):
-        return pltpu.make_async_remote_copy(src, dst, s, r, device_id={"view": peer}, device_id_type=MESH)
-
-    def over_gauss(peer, src, dst, s, r):
-        return pltpu.make_async_remote_copy(src, dst, s, r, device_id={"gauss": peer}, device_id_type=MESH)
-
-    def owner(i):
-        return ((gy + i // 8) % 4) * 8 + (gz + i % 8) % 8
-
-    def tell(i, slot):
-        return over_gauss((g + i) % NG, count, counts.at[slot], s_count.at[i], r_count.at[slot])
-
-    def give_part(i, slot):
-        peer = (v + i) % NV
-        return over_view(peer, part.at[peer], taken.at[slot], s_part.at[i], r_part.at[slot])
-
-    def give_best(i, slot):
-        return over_view((v + i) % NV, merged, best.at[slot], s_best.at[i], r_best.at[slot])
-
-    def give_pack(i, slot):
-        peer = (v + i) % NV
-        return over_view(peer, turnedp.at[pl.ds(peer * 16, 16)], takenp.at[slot], s_pack.at[i], r_pack.at[slot])
-
-    def give_top(t):
-        at = pl.ds(t * PER, PER)
-        return over_gauss(owner(v * 4 + t), mergedp.at[at], top.at[at], s_top.at[t], r_top.at[t])
-
-    each(1, NG, lambda i: tell(i, g).start())
-    each(1, NV, lambda i: give_part(i, v).start())
-    counts[g] = count[...]
-    each(1, NG, lambda i: tell(i, (g + i) % NG).wait_recv())
-
-    def add(s, mine):
-        return mine + jnp.where(s < g, (counts[s] + (BLK - 1)) >> 7, 0)
-
-    tab[...] = lax.fori_loop(0, NG, add, jnp.zeros((8, 128), jnp.int32))
-    to_smem = pltpu.make_async_copy(tab, stab, own.at[0])
-    to_smem.start()
-    to_smem.wait()
-    shift = stab[0, 0]
-
-    def pair(i):
-        at = pl.ds(i * PER, PER)
-        return over_gauss(owner(i), turned.at[at], mine.at[at], s_pair.at[i], r_pair.at[i])
-
-    keep = pltpu.make_async_copy(turned.at[0:PER], mine.at[0:PER], own.at[1])
-
-    def turn(i):
-        block = (owner(i) - shift) & (NG - 1)
-        for w in range(PER):
-            turned[i * PER + w] = tiles[block + w * NG]
-            turnedp[i * PER + w] = packed[block + w * NG]
-
-    each(0, NG, turn)
-    each(1, NG, lambda i: pair(i).start())
-    keep.start()
-    each(1, NV, lambda i: give_pack(i, v).start())
-
-    def first():
-        each(1, NV, lambda i: give_part(i, (v + i) % NV).wait_recv())
-        so_far = lax.fori_loop(1, NV, lambda i, so: jnp.maximum(so, taken[(v + i) % NV]), part[v])
-        merged[...] = so_far
-        best[v] = so_far
-        each(1, NV, lambda i: give_best(i, v).start())
-
-    def second():
-        each(1, NV, lambda i: give_pack(i, (v + i) % NV).wait_recv())
-        best_p = lax.fori_loop(1, NV, lambda i, so: jnp.maximum(so, takenp[(v + i) % NV]), turnedp[pl.ds(v * 16, 16)])
-        mergedp[...] = best_p
-
-        @pl.when(v > 0)
-        def _():
-            give_top(0).start()
-
-        @pl.when(v == 0)
-        def _():
-            top[0:PER] = best_p[0:PER]
-
-        each(1, 4, lambda t: give_top(t).start())
-
-    def third():
-        @pl.when(v > 0)
-        def _():
-            give_top(0).wait_recv()
-
-        each(1, 4, lambda t: give_top(t).wait_recv())
-
-    first()
-
-    sub = lax.broadcasted_iota(jnp.int32, (8, 128), 0)
-    k = lax.broadcasted_iota(jnp.int32, (8, 128), 1) * NG + g
-    off = jnp.zeros((8, 128), jnp.int32)
-    every = jnp.zeros((8, 128), jnp.int32)
-    source = jnp.zeros((8, 128), jnp.int32)
-    for s in range(NG):
-        n = counts[s]
-        blocks = (n + (BLK - 1)) >> 7
-        where = (((gy - s // 8) & 3) * 8 + ((gz - s % 8) & 7)) * PER
-        inside = (k >= off) & (k < off + blocks)
-        source = jnp.where(inside, where + ((k - off) >> 5), source)
-        off = off + blocks
-        every = every + n
-    slots = (off - g + (NG - 1)) >> 5
-    most = (off + (NG - 1)) >> 5
-    pick = sum((most > size).astype(jnp.int32) for size in SIZES[:-1])
-    table[...] = jnp.where(sub == 0, source, jnp.where(sub == 1, every, slots))
-    tab[...] = pick
-    pick_smem = pltpu.make_async_copy(tab, stab, own.at[0])
-    pick_smem.start()
-
-    second()
-    third()
-    pick_smem.wait()
-    kind[0, 0] = stab[0, 0]
-    keep.wait()
-    each(1, NG, lambda i: pair(i).wait_recv())
-    each(1, NV, lambda i: give_best(i, (v + i) % NV).wait_recv())
-
-    each(1, NG, lambda i: tell(i, g).wait_send())
-    each(1, NG, lambda i: pair(i).wait_send())
-    each(1, NV, lambda i: give_part(i, v).wait_send())
-    each(1, NV, lambda i: give_pack(i, v).wait_send())
-    each(1, NV, lambda i: give_best(i, v).wait_send())
-
-    @pl.when(v > 0)
-    def _():
-        give_top(0).wait_send()
-
-    each(1, 4, lambda t: give_top(t).wait_send())
-
-
-def share_kernel(size, mine, table, top, out, peaks, s_own, r_own, s_side, r_side, s_far, r_far, s_peak, r_peak, own):
+def spread(out, size, source, mine, s_own, r_own, s_side, r_side, s_far, r_far, ready):
     v = lax.axis_index("view")
     core, chip = v % 2, v // 2
     mate = chip * 2 + 1 - core
     right, left, far = (((chip + i) % 4) * 2 + core for i in (1, 3, 2))
-    barrier = pltpu.get_barrier_semaphore()
-    each(1, NV, lambda i: pl.semaphore_signal(barrier, inc=1, device_id={"view": (v + i) % NV}, device_id_type=MESH))
     rows = pl.ds(pl.multiple_of(v * 8, 8), 8)
 
-    def cols(at):
-        return pl.ds(pl.multiple_of(at * BLK, BLK), BLK)
-
-    def place(q):
-        out[rows, cols(q)] = mine[table[0, q]]
-
-    each(0, size, place)
-    keep = pltpu.make_async_copy(top, peaks.at[pl.ds(v * 16, 16)], own.at[0])
-    keep.start()
-    pl.semaphore_wait(barrier, NV - 1)
+    def place(q, _):
+        out[rows, pl.ds(pl.multiple_of(q * BLK, BLK), BLK)] = mine[source(q)]
+        return 0
+
+    lax.fori_loop(0, size, place, 0, unroll=4)
+    ready()
     wide = size * BLK // CHUNKS
 
     def over_view(peer, group, c, s, r):
@@ -404,17 +253,6 @@
         go(0, c, v).start()
         go(1, c, v).start()
         side(0, c, v).start()
-    def give_peak(i, slot):
-        return pltpu.make_async_remote_copy(
-            top,
-            peaks.at[pl.ds(slot * 16, 16)],
-            s_peak.at[i],
-            r_peak.at[slot],
-            device_id={"view": (v + i) % NV},
-            device_id_type=MESH,
-        )
-
-    each(1, NV, lambda i: give_peak(i, v).start())
     for c in range(CHUNKS):
         go(0, c, left).wait_recv()
         if c < CHUNKS // 2:
@@ -435,13 +273,175 @@
         go(0, c, v).wait_send()
         go(1, c, v).wait_send()
         on(0, c, v).wait_send()
+
+
+def move_kernel(
+    part, packed, tiles, count,
+    mine, out, peaks, best, counts, table, kind,
+    taken, takenp, merged, mergedp, top, turned, turnedp, tab, stab,
+    s_part, r_part, s_pack, r_pack, s_best, r_best, s_peak, r_peak, s_count, r_count, s_pair, r_pair, s_top, r_top,
+    s_own, r_own, s_side, r_side, s_far, r_far, own,
+):
+    v, g = lax.axis_index("view"), lax.axis_index("gauss")
+    gy, gz = g // 8, g % 8
+    barrier = pltpu.get_barrier_semaphore()
+    each(1, NV, lambda i: pl.semaphore_signal(barrier, inc=1, device_id={"view": (v + i) % NV}, device_id_type=MESH))
+    each(1, NG, lambda i: pl.semaphore_signal(barrier, inc=1, device_id={"gauss": (g + i) % NG}, device_id_type=MESH))
+    pl.semaphore_wait(barrier, NV - 1 + NG - 1)
+
+    def over_view(peer, src, dst, s, r):
+        return pltpu.make_async_remote_copy(src, dst, s, r, device_id={"view": peer}, device_id_type=MESH)
+
+    def over_gauss(peer, src, dst, s, r):
+        return pltpu.make_async_remote_copy(src, dst, s, r, device_id={"gauss": peer}, device_id_type=MESH)
+
+    def owner(i):
+        return ((gy + i // 8) % 4) * 8 + (gz + i % 8) % 8
+
+    def tell(i, slot):
+        return over_gauss((g + i) % NG, count, counts.at[slot], s_count.at[i], r_count.at[slot])
+
+    def give_part(i, slot):
+        peer = (v + i) % NV
+        return over_view(peer, part.at[peer], taken.at[slot], s_part.at[i], r_part.at[slot])
+
+    def give_best(i, slot):
+        return over_view((v + i) % NV, merged, best.at[slot], s_best.at[i], r_best.at[slot])
+
+    def give_pack(i, slot):
+        peer = (v + i) % NV
+        return over_view(peer, turnedp.at[pl.ds(peer * 16, 16)], takenp.at[slot], s_pack.at[i], r_pack.at[slot])
+
+    def give_top(t):
+        at = pl.ds(t * PER, PER)
+        return over_gauss(owner(v * 4 + t), mergedp.at[at], top.at[at], s_top.at[t], r_top.at[t])
+
+    each(1, NG, lambda i: tell(i, g).start())
+    each(1, NV, lambda i: give_part(i, v).start())
+    counts[g] = count[...]
+    each(1, NG, lambda i: tell(i, (g + i) % NG).wait_recv())
+
+    def add(s, mine):
+        return mine + jnp.where(s < g, (counts[s] + (BLK - 1)) >> 7, 0)
+
+    tab[...] = lax.fori_loop(0, NG, add, jnp.zeros((8, 128), jnp.int32))
+    to_smem = pltpu.make_async_copy(tab, stab, own.at[0])
+    to_smem.start()
+    to_smem.wait()
+    shift = stab[0, 0]
+
+    def pair(i):
+        at = pl.ds(i * PER, PER)
+        return over_gauss(owner(i), turned.at[at], mine.at[at], s_pair.at[i], r_pair.at[i])
+
+    keep = pltpu.make_async_copy(turned.at[0:PER], mine.at[0:PER], own.at[1])
+
+    def turn(i):
+        block = (owner(i) - shift) & (NG - 1)
+        for w in range(PER):
+            turned[i * PER + w] = tiles[block + w * NG]
+            turnedp[i * PER + w] = packed[block + w * NG]
+
+    each(0, NG, turn)
+    each(1, NG, lambda i: pair(i).start())
+    keep.start()
+    each(1, NV, lambda i: give_pack(i, v).start())
+
+    def first():
+        each(1, NV, lambda i: give_part(i, (v + i) % NV).wait_recv())
+        so_far = lax.fori_loop(1, NV, lambda i, so: jnp.maximum(so, taken[(v + i) % NV]), part[v])
+        merged[...] = so_far
+        best[v] = so_far
+        each(1, NV, lambda i: give_best(i, v).start())
+
+    def second():
+        each(1, NV, lambda i: give_pack(i, (v + i) % NV).wait_recv())
+        best_p = lax.fori_loop(1, NV, lambda i, so: jnp.maximum(so, takenp[(v + i) % NV]), turnedp[pl.ds(v * 16, 16)])
+        mergedp[...] = best_p
+
+        @pl.when(v > 0)
+        def _():
+            give_top(0).start()
+
+        @pl.when(v == 0)
+        def _():
+            top[0:PER] = best_p[0:PER]
+
+        each(1, 4, lambda t: give_top(t).start())
+
+    def third():
+        @pl.when(v > 0)
+        def _():
+            give_top(0).wait_recv()
+
+        each(1, 4, lambda t: give_top(t).wait_recv())
+
+    first()
+
+    sub = lax.broadcasted_iota(jnp.int32, (8, 128), 0)
+    k = lax.broadcasted_iota(jnp.int32, (8, 128), 1) * NG + g
+    off = jnp.zeros((8, 128), jnp.int32)
+    every = jnp.zeros((8, 128), jnp.int32)
+    source = jnp.zeros((8, 128), jnp.int32)
+    for s in range(NG):
+        n = counts[s]
+        blocks = (n + (BLK - 1)) >> 7
+        where = (((gy - s // 8) & 3) * 8 + ((gz - s % 8) & 7)) * PER
+        inside = (k >= off) & (k < off + blocks)
+        source = jnp.where(inside, where + ((k - off) >> 5), source)
+        off = off + blocks
+        every = every + n
+    slots = (off - g + (NG - 1)) >> 5
+    most = (off + (NG - 1)) >> 5
+    more = (most > FIRST).astype(jnp.int32)
+    filled = jnp.where(sub == 0, source, jnp.where(sub == 1, every, jnp.where(sub == 2, slots, more)))
+    table[...] = filled
+    tab[...] = filled
+    pick_smem = pltpu.make_async_copy(tab, stab, own.at[0])
+    pick_smem.start()
+
+    second()
+    third()
+    pick_smem.wait()
+    kind[0, 0] = stab[3, 0]
+
+    def give_peak(i, slot):
+        at = peaks.at[pl.ds(slot * 16, 16)]
+        return over_view((v + i) % NV, top, at, s_peak.at[i], r_peak.at[slot])
+
+    each(1, NV, lambda i: give_peak(i, v).start())
+    peaks[pl.ds(v * 16, 16)] = top[...]
+    keep.wait()
+    each(1, NG, lambda i: pair(i).wait_recv())
+    spread(
+        out, FIRST, lambda q: stab[0, q], mine, s_own, r_own, s_side, r_side, s_far, r_far, lambda: None
+    )
     each(1, NV, lambda i: give_peak(i, (v + i) % NV).wait_recv())
     each(1, NV, lambda i: give_peak(i, v).wait_send())
-    keep.wait()
-
-
-def lay_kernel(size, table, best, peaks, tiles, blank, clones, peak, total, stage, sem):
-    del blank
+    each(1, NV, lambda i: give_best(i, (v + i) % NV).wait_recv())
+
+    each(1, NG, lambda i: tell(i, g).wait_send())
+    each(1, NG, lambda i: pair(i).wait_send())
+    each(1, NV, lambda i: give_part(i, v).wait_send())
+    each(1, NV, lambda i: give_pack(i, v).wait_send())
+    each(1, NV, lambda i: give_best(i, v).wait_send())
+
+    @pl.when(v > 0)
+    def _():
+        give_top(0).wait_send()
+
+    each(1, 4, lambda t: give_top(t).wait_send())
+
+
+def share_kernel(mine, table, out, *sems):
+    v = lax.axis_index("view")
+    barrier = pltpu.get_barrier_semaphore()
+    each(1, NV, lambda i: pl.semaphore_signal(barrier, inc=1, device_id={"view": (v + i) % NV}, device_id_type=MESH))
+    spread(out, CAP - FIRST, lambda q: table[0, FIRST + q], mine, *sems, lambda: pl.semaphore_wait(barrier, NV - 1))
+
+
+def lay_kernel(more, table, best, peaks, tiles, *refs):
+    rest, _, clones, peak, total, stage, sem = refs if more else (None, *refs)
     sub = lax.broadcasted_iota(jnp.int32, (8, 128), 0)
     used = table[2, 0]
     total[0, 0] = table[1, 0]
@@ -449,26 +449,42 @@
     def cols(at):
         return pl.ds(pl.multiple_of(at * BLK, BLK), BLK)
 
-    def copies(src, dst, sem):
-        for n in (128, 64, 32, 16, 8, 4, 2, 1):
-            at = pl.ds(pl.multiple_of((used & (256 - 2 * n)) * BLK, BLK), n * BLK)
-            if n <= size:
-                yield (used & n) != 0, pltpu.make_async_copy(src.at[:, at], dst.at[:, at], sem)
-
-    main = list(copies(tiles.at[0:56, :], clones.at[0:56, :], sem.at[0]))
-    rest = list(copies(stage.at[0 : ROWS - 56, :], clones.at[56:ROWS, :], sem.at[1]))
+    def runs(count, most):
+        for n in (64, 32, 16, 8, 4, 2, 1):
+            if n <= most:
+                yield (count & n) != 0, pl.multiple_of((count & (256 - 2 * n)) * BLK, BLK), n * BLK
+
+    if more:
+        pieces = [(tiles, 0, (True, 0, FIRST * BLK))]
+        pieces += [(rest, FIRST, run) for run in runs(used - FIRST, CAP - FIRST)]
+    else:
+        pieces = [(tiles, 0, run) for run in runs(used, FIRST)]
+    main, last = [], []
+    for src, first, (on, at, size) in pieces:
+        to = pl.multiple_of(at + first * BLK, BLK)
+        main.append((on, pltpu.make_async_copy(
+            src.at[0:56, pl.ds(at, size)], clones.at[0:56, pl.ds(to, size)], sem.at[0]
+        )))
+        last.append((on, pltpu.make_async_copy(
+            stage.at[0 : ROWS - 56, pl.ds(to, size)], clones.at[56:ROWS, pl.ds(to, size)], sem.at[1]
+        )))
     for on, copy in main:
         pl.when(on)(copy.start)
 
-    def finish(q):
-        tops = peaks[table[0, q]]
-        gtop = jnp.broadcast_to(jnp.sqrt(tops[0:1]), (8, 128))
-        ltop = jnp.broadcast_to(3.0 * jnp.sqrt(tops[1:2]), (8, 128))
-        tile = tiles[56:64, cols(q)]
-        stage[:, cols(q)] = jnp.where(sub == 3, gtop, jnp.where(sub == 4, ltop, tile))
-
-    each(0, used, finish)
-    for on, copy in rest:
+    def finish(src, first):
+        def one(q):
+            tops = peaks[table[0, q]]
+            gtop = jnp.broadcast_to(jnp.sqrt(tops[0:1]), (8, 128))
+            ltop = jnp.broadcast_to(3.0 * jnp.sqrt(tops[1:2]), (8, 128))
+            tile = src[56:64, cols(q - first)]
+            stage[:, cols(q)] = jnp.where(sub == 3, gtop, jnp.where(sub == 4, ltop, tile))
+
+        return one
+
+    each(jnp.int32(0), jnp.minimum(used, FIRST), finish(tiles, 0))
+    if more:
+        each(jnp.int32(FIRST), used, finish(rest, FIRST))
+    for on, copy in last:
         pl.when(on)(copy.start)
 
     def roots(c, _):
@@ -479,7 +495,7 @@
         return 0
 
     lax.fori_loop(0, 16, roots, 0)
-    for on, copy in main + rest:
+    for on, copy in main + last:
         pl.when(on)(copy.wait)
 
 
@@ -487,6 +503,7 @@
     f32, i32 = jnp.float32, jnp.int32
     shape = jax.ShapeDtypeStruct
     dma = pltpu.SemaphoreType.DMA
+    view_sems = [dma((2, CHUNKS))] * 2 + [dma((4, CHUNKS))] * 2 + [dma((CHUNKS,))] * 2
     mask = clone_mask.reshape(128, 128)
     part, packed, tiles, count, blank = pl.pallas_call(
         front_kernel,
@@ -530,13 +547,14 @@
         )
     )
 
-    mine, top, best, _, table, kind = pl.pallas_call(
+    mine, out, peaks, best, _, table, kind = pl.pallas_call(
         move_kernel,
         in_specs=[VMEM] * 4,
-        out_specs=(VMEM,) * 5 + (SMEM,),
+        out_specs=(VMEM,) * 6 + (SMEM,),
         out_shape=(
             shape((CAP, 8, 128), f32),
-            shape((16, 2, 128), f32),
+            shape((8 * NV, FIRST * BLK), f32),
+            shape((CAP, 2, 128), f32),
             shape((NV, 2, 16, 128), f32),
             shape((NG, 8, 128), i32),
             shape((8, 128), i32),
@@ -547,14 +565,16 @@
             pltpu.VMEM((NV, 16, 2, 128), f32),
             pltpu.VMEM((2, 16, 128), f32),
             pltpu.VMEM((16, 2, 128), f32),
+            pltpu.VMEM((16, 2, 128), f32),
             pltpu.VMEM((CAP, 8, 128), f32),
             pltpu.VMEM((CAP, 2, 128), f32),
             pltpu.VMEM((8, 128), i32),
             pltpu.SMEM((8, 128), i32),
         ]
-        + [dma((NV,))] * 6
+        + [dma((NV,))] * 8
         + [dma((NG,))] * 4
         + [dma((4,))] * 2
+        + view_sems
         + [dma((2,))],
         compiler_params=pltpu.CompilerParams(
             collective_id=0, has_side_effects=True, vmem_limit_bytes=16 * 2**20
@@ -562,41 +582,39 @@
         name="move",
     )(part, packed, tiles, count)
 
-    def share(n, size):
-        gather = pl.pallas_call(
-            functools.partial(share_kernel, size),
-            in_specs=[VMEM, SMEM, VMEM],
-            out_specs=(VMEM, VMEM),
-            out_shape=(shape((8 * NV, size * BLK), f32), shape((CAP, 2, 128), f32)),
-            scratch_shapes=[dma((2, CHUNKS))] * 2
-            + [dma((4, CHUNKS))] * 2
-            + [dma((CHUNKS,))] * 2
-            + [dma((NV,))] * 2
-            + [dma((1,))],
-            compiler_params=pltpu.CompilerParams(
-                collective_id=1 + n, has_side_effects=True, vmem_limit_bytes=16 * 2**20
-            ),
-            name=f"share{size}",
-        )
-        lay = pl.pallas_call(
-            functools.partial(lay_kernel, size),
-            in_specs=[SMEM, VMEM, VMEM, VMEM, HBM],
+    share = pl.pallas_call(
+        share_kernel,
+        in_specs=[VMEM, SMEM],
+        out_specs=VMEM,
+        out_shape=shape((8 * NV, (CAP - FIRST) * BLK), f32),
+        scratch_shapes=view_sems,
+        compiler_params=pltpu.CompilerParams(
+            collective_id=1, has_side_effects=True, vmem_limit_bytes=16 * 2**20
+        ),
+        name="share",
+    )
+
+    def lay(more, table, best, peaks, *tiles_and_blank):
+        return pl.pallas_call(
+            functools.partial(lay_kernel, more),
+            in_specs=[SMEM, VMEM, VMEM] + [VMEM] * (1 + more) + [HBM],
             out_specs=(HBM, VMEM, SMEM),
             out_shape=(shape((ROWS, G), f32), shape((2, G), f32), shape((1, 1), i32)),
-            input_output_aliases={4: 0},
-            scratch_shapes=[pltpu.VMEM((8, size * BLK), f32), dma((2,))],
+            input_output_aliases={4 + more: 0},
+            scratch_shapes=[pltpu.VMEM((8, G), f32), dma((2,))],
             compiler_params=pltpu.CompilerParams(vmem_limit_bytes=16 * 2**20),
-            name=f"lay{size}",
-        )
-        def branch(mine, table, best, top, blank):
-            tiles, peaks = gather(mine, table, top)
-            return lay(table, best, peaks, tiles, pltpu.with_memory_space_constraint(blank, pltpu.HBM))
-
-        return branch
+            name="lay_more" if more else "lay",
+        )(table, best, peaks, *tiles_and_blank)
+
+    def few(mine, table, best, peaks, out, blank):
+        return lay(False, table, best, peaks, out, pltpu.with_memory_space_constraint(blank, pltpu.HBM))
+
+    def many(mine, table, best, peaks, out, blank):
+        rest = share(mine, table)
+        return lay(True, table, best, peaks, out, rest, pltpu.with_memory_space_constraint(blank, pltpu.HBM))
 
     blank = pltpu.with_memory_space_constraint(blank, pltpu.HBM)
-    branches = [share(n, size) for n, size in enumerate(SIZES)]
-    clones, peak, total = lax.switch(kind.reshape(()), branches, mine, table, best, top, blank)
+    clones, peak, total = lax.switch(kind.reshape(()), [few, many], mine, table, best, peaks, out, blank)
     return (peak, clones, total.reshape(()))
 
 

time: 61.1 us -> 58.3 us (0.954)
  Pallas kernels: 59.6 us -> 56.4 us
    pallas_call x3 -> x2, Pallas kernels: 54 us -> 50.9 us  [the longest x1 48.3 us: body(): pl.pallas_call(move_kernel, in_specs=[VMEM] * 4, out_specs=(VMEM,) * 6 +...]
where the time goes in v5:
time: 58.3 us; the launch traced here: 57.7 us
  Pallas kernels  56.4 us (97%)
  between operations  1.28 us (2%)
    pallas_call x1, Pallas kernels, body(): pl.pallas_call(move_kernel, in_specs=[VMEM] * 4, out_specs=(VMEM,) * 6 +...  48.3 us
    pallas_call x1, Pallas kernels, body(): pl.pallas_call(front_kernel, in_specs=[HBM] * 10, out_specs=(VMEM,) * 4 +...  5.55 us
    pallas_call x1, Pallas kernels, lay(): pl.pallas_call(functools.partial(lay_kernel, more), in_specs=[SMEM, VMEM,...  2.57 us

profile of v5, /device:TPU:1, one launch (start us, length us, event | category | flops | bytes accessed | tf_op | source)
XLA Modules:
  0.0 57.7 jit_solution(4518581508172143057)
XLA Ops:
  0.6 5.5 %front.1 = (f32[8,2,16,128]{3,2,1,0:T(8,128)S(1)}, f32[128,2,128]{2,1,0:T(2,128)S(1)}, f32[128,8,128]{2,1,0:T(8,128)S(1)}, s32[8,128]{1,0:T(8,128)S(1)}, f32[61,16384]{1,0:T(8,128)}) custom-call(s32[128,128]{1,0:T(8,128)} %bitcast.5, f32[3,16384]{1,0:T(4,128)} %means_h.1, f32[3,16384]{1,0:T(4,128)} %scales_h.1, f32[4,16384]{1,0:T(4,128)} %quats_h.1, ...), custom_call_target="tpu_custom_call" | custom-call | tf_op jit(solution)/shard_map/front/pallas_call | solution.py:508
  6.2 48.3 %move.1 = (f32[128,8,128]{2,1,0:T(8,128)S(1)}, f32[64,7680]{1,0:T(8,128)S(1)}, f32[128,2,128]{2,1,0:T(2,128)S(1)}, f32[8,2,16,128]{3,2,1,0:T(8,128)S(1)}, s32[32...) custom-call(f32[8,2,16,128]{3,2,1,0:T(8,128)S(1)} %get-tuple-element.63.part, ...), custom_call_target="tpu_custom_call" | custom-call | tf_op jit(solution)/shard_map/move/pallas_call | solution.py:550
  55.1 2.6 %conditional.1 = (f32[61,16384]{1,0:T(8,128)}, f32[2,16384]{1,0:T(2,128)}, s32[]{:T(128)}) conditional(s32[]{:T(128)} %bitcast.4, (s32[8,128]{1,0:T(8,128)S(1)}, f32[8,2,16,128]{3,2,1,0:T(8,128)S(1)}, f32[128,2,128]{2,1,0:T(2,128)S(1)}, f32[64,7680]{1,0:T(8,128)S(1)}, f32[61,16384]{1,0:T(8,128)}) %tuple.18, (f32[128,8,128]{2,1,0:T(8,128)S(1)}, ...), branch_computations={%region_0.0_spmd, %region_1.0_spmd} | conditional | bytes 24 | solution.py:617
  55.1 2.6 %lay.1 = (f32[61,16384]{1,0:T(8,128)}, f32[2,16384]{1,0:T(2,128)}, s32[1,1]{1,0:T(1,128)}) custom-call(s32[8,128]{1,0:T(8,128)S(1)} %get-tuple-element.29.table, f32[8,2,16,128]{3,2,1,0:T(8,128)S(1)} %get-tuple-element.30.best, f32[128,2,128]{2,1,0:T(2,128)S(1)} %get-tuple-element.31.peaks, ...), custom_call_target="tpu_custom_call", output_to_operand_aliasing={{0}: (4, {})} | custom-call | tf_op jit(solution)/shard_map/cond/branch_0_fun/lay/pallas_call | solution.py:598

commit v6 on v5

--- a/solution.py
+++ b/solution.py
@@ -156,7 +156,7 @@
         gl[1:2, s] = lbest.reshape(1, 1024)
         return 0
 
-    lax.fori_loop(0, 16, step, 0)
+    lax.fori_loop(0, 16, step, 0, unroll=4)
 
     load_a.wait()
 
@@ -209,7 +209,7 @@
         return done[0][1], done[1][1]
 
     zero = jnp.zeros((8, 128), jnp.float32)
-    left = lax.fori_loop(0, 128, pack, (zero, zero), unroll=8)
+    left = lax.fori_loop(0, 128, pack, (zero, zero), unroll=32)
     last = stab[1, 127]
 
     @pl.when(last < G)
@@ -342,8 +342,11 @@
             turned[i * PER + w] = tiles[block + w * NG]
             turnedp[i * PER + w] = packed[block + w * NG]
 
-    each(0, NG, turn)
-    each(1, NG, lambda i: pair(i).start())
+    for i in range(NG + 2):
+        if i < NG:
+            turn(i)
+        if i > 2:
+            pair(i - 2).start()
     keep.start()
     each(1, NV, lambda i: give_pack(i, v).start())
 

time: 58.3 us -> 57.1 us (0.979)
  Pallas kernels: 56.4 us -> 55.2 us
    pallas_call x1, Pallas kernels: 5.55 us -> 4.54 us  [body(): pl.pallas_call(front_kernel, in_specs=[HBM] * 10, out_specs=(VMEM,) * 4 +...]
where the time goes in v6:
time: 57.1 us; the launch traced here: 56.5 us
  Pallas kernels  55.2 us (97%)
  between operations  1.28 us (2%)
    pallas_call x1, Pallas kernels, body(): pl.pallas_call(move_kernel, in_specs=[VMEM] * 4, out_specs=(VMEM,) * 6 +...  48.2 us
    pallas_call x1, Pallas kernels, body(): pl.pallas_call(front_kernel, in_specs=[HBM] * 10, out_specs=(VMEM,) * 4 +...  4.54 us
    pallas_call x1, Pallas kernels, lay(): pl.pallas_call(functools.partial(lay_kernel, more), in_specs=[SMEM, VMEM,...  2.53 us

profile of v6, /device:TPU:1, one launch (start us, length us, event | category | flops | bytes accessed | tf_op | source)
XLA Modules:
  0.0 56.5 jit_solution(8015229301762975475)
XLA Ops:
  0.6 4.5 %front.1 = (f32[8,2,16,128]{3,2,1,0:T(8,128)S(1)}, f32[128,2,128]{2,1,0:T(2,128)S(1)}, f32[128,8,128]{2,1,0:T(8,128)S(1)}, s32[8,128]{1,0:T(8,128)S(1)}, f32[61,16384]{1,0:T(8,128)}) custom-call(s32[128,128]{1,0:T(8,128)} %bitcast.5, f32[3,16384]{1,0:T(4,128)} %means_h.1, f32[3,16384]{1,0:T(4,128)} %scales_h.1, f32[4,16384]{1,0:T(4,128)} %quats_h.1, ...), custom_call_target="tpu_custom_call" | custom-call | tf_op jit(solution)/shard_map/front/pallas_call | solution.py:511
  5.2 48.2 %move.1 = (f32[128,8,128]{2,1,0:T(8,128)S(1)}, f32[64,7680]{1,0:T(8,128)S(1)}, f32[128,2,128]{2,1,0:T(2,128)S(1)}, f32[8,2,16,128]{3,2,1,0:T(8,128)S(1)}, s32[32...) custom-call(f32[8,2,16,128]{3,2,1,0:T(8,128)S(1)} %get-tuple-element.63.part, ...), custom_call_target="tpu_custom_call" | custom-call | tf_op jit(solution)/shard_map/move/pallas_call | solution.py:553
  54.0 2.6 %conditional.1 = (f32[61,16384]{1,0:T(8,128)}, f32[2,16384]{1,0:T(2,128)}, s32[]{:T(128)}) conditional(s32[]{:T(128)} %bitcast.4, (s32[8,128]{1,0:T(8,128)S(1)}, f32[8,2,16,128]{3,2,1,0:T(8,128)S(1)}, f32[128,2,128]{2,1,0:T(2,128)S(1)}, f32[64,7680]{1,0:T(8,128)S(1)}, f32[61,16384]{1,0:T(8,128)}) %tuple.18, (f32[128,8,128]{2,1,0:T(8,128)S(1)}, ...), branch_computations={%region_0.0_spmd, %region_1.0_spmd} | conditional | bytes 24 | solution.py:620
  54.0 2.5 %lay.1 = (f32[61,16384]{1,0:T(8,128)}, f32[2,16384]{1,0:T(2,128)}, s32[1,1]{1,0:T(1,128)}) custom-call(s32[8,128]{1,0:T(8,128)S(1)} %get-tuple-element.29.table, f32[8,2,16,128]{3,2,1,0:T(8,128)S(1)} %get-tuple-element.30.best, f32[128,2,128]{2,1,0:T(2,128)S(1)} %get-tuple-element.31.peaks, ...), custom_call_target="tpu_custom_call", output_to_operand_aliasing={{0}: (4, {})} | custom-call | tf_op jit(solution)/shard_map/cond/branch_0_fun/lay/pallas_call | solution.py:601

commit v7 on v6

--- a/solution.py
+++ b/solution.py
@@ -232,8 +232,6 @@
         out[rows, pl.ds(pl.multiple_of(q * BLK, BLK), BLK)] = mine[source(q)]
         return 0
 
-    lax.fori_loop(0, size, place, 0, unroll=4)
-    ready()
     wide = size * BLK // CHUNKS
 
     def over_view(peer, group, c, s, r):
@@ -249,10 +247,16 @@
     def on(way, c, group):
         return over_view(right if way == 0 else left, group, c, s_far.at[c], r_far.at[c])
 
-    for c in range(CHUNKS):
-        go(0, c, v).start()
-        go(1, c, v).start()
-        side(0, c, v).start()
+    per = size // CHUNKS
+    for c in range(CHUNKS + 1):
+        if c < CHUNKS:
+            lax.fori_loop(c * per, (c + 1) * per, place, 0, unroll=True)
+        if c == 0:
+            ready()
+        else:
+            go(0, c - 1, v).start()
+            go(1, c - 1, v).start()
+            side(0, c - 1, v).start()
     for c in range(CHUNKS):
         go(0, c, left).wait_recv()
         if c < CHUNKS // 2:

time: 57.1 us -> 57.2 us (level)
  no operation moved by 1% of the time
where the time goes in v7:
time: 57.2 us; the launch traced here: 56.7 us
  Pallas kernels  55.4 us (97%)
  between operations  1.28 us (2%)
    pallas_call x1, Pallas kernels, body(): pl.pallas_call(move_kernel, in_specs=[VMEM] * 4, out_specs=(VMEM,) * 6 +...  48.2 us
    pallas_call x1, Pallas kernels, body(): pl.pallas_call(front_kernel, in_specs=[HBM] * 10, out_specs=(VMEM,) * 4 +...  4.54 us
    pallas_call x1, Pallas kernels, lay(): pl.pallas_call(functools.partial(lay_kernel, more), in_specs=[SMEM, VMEM,...  2.7 us

profile of v7, /device:TPU:1, one launch (start us, length us, event | category | flops | bytes accessed | tf_op | source)
XLA Modules:
  0.0 56.7 jit_solution(5949582003613725927)
XLA Ops:
  0.6 4.5 %front.1 = (f32[8,2,16,128]{3,2,1,0:T(8,128)S(1)}, f32[128,2,128]{2,1,0:T(2,128)S(1)}, f32[128,8,128]{2,1,0:T(8,128)S(1)}, s32[8,128]{1,0:T(8,128)S(1)}, f32[61,16384]{1,0:T(8,128)}) custom-call(s32[128,128]{1,0:T(8,128)} %bitcast.5, f32[3,16384]{1,0:T(4,128)} %means_h.1, f32[3,16384]{1,0:T(4,128)} %scales_h.1, f32[4,16384]{1,0:T(4,128)} %quats_h.1, ...), custom_call_target="tpu_custom_call" | custom-call | tf_op jit(solution)/shard_map/front/pallas_call | solution.py:515
  5.2 48.2 %move.1 = (f32[128,8,128]{2,1,0:T(8,128)S(1)}, f32[64,7680]{1,0:T(8,128)S(1)}, f32[128,2,128]{2,1,0:T(2,128)S(1)}, f32[8,2,16,128]{3,2,1,0:T(8,128)S(1)}, s32[32...) custom-call(f32[8,2,16,128]{3,2,1,0:T(8,128)S(1)} %get-tuple-element.63.part, ...), custom_call_target="tpu_custom_call" | custom-call | tf_op jit(solution)/shard_map/move/pallas_call | solution.py:557
  54.0 2.7 %conditional.1 = (f32[61,16384]{1,0:T(8,128)}, f32[2,16384]{1,0:T(2,128)}, s32[]{:T(128)}) conditional(s32[]{:T(128)} %bitcast.4, (s32[8,128]{1,0:T(8,128)S(1)}, f32[8,2,16,128]{3,2,1,0:T(8,128)S(1)}, f32[128,2,128]{2,1,0:T(2,128)S(1)}, f32[64,7680]{1,0:T(8,128)S(1)}, f32[61,16384]{1,0:T(8,128)}) %tuple.18, (f32[128,8,128]{2,1,0:T(8,128)S(1)}, ...), branch_computations={%region_0.0_spmd, %region_1.0_spmd} | conditional | bytes 24 | solution.py:624
  54.0 2.7 %lay.1 = (f32[61,16384]{1,0:T(8,128)}, f32[2,16384]{1,0:T(2,128)}, s32[1,1]{1,0:T(1,128)}) custom-call(s32[8,128]{1,0:T(8,128)S(1)} %get-tuple-element.29.table, f32[8,2,16,128]{3,2,1,0:T(8,128)S(1)} %get-tuple-element.30.best, f32[128,2,128]{2,1,0:T(2,128)S(1)} %get-tuple-element.31.peaks, ...), custom_call_target="tpu_custom_call", output_to_operand_aliasing={{0}: (4, {})} | custom-call | tf_op jit(solution)/shard_map/cond/branch_0_fun/lay/pallas_call | solution.py:605
